TPU v7x, 512 devices: a whole 4x4x16 slice. The times are simulated.
512 devices in a mesh: inline: 32 (over z, y_hi), xline: 16 (over y_lo, x, core).
Axes of the slice: x: 4, y: 4 (y_hi: 2, y_lo: 2; y = y_hi * 2 + y_lo), z: 16, core: 2. Of those that a mesh axis runs over, the one named last changes fastest.
Arguments:
- samples: float32 [2, 32, 16384], P(None, 'inline', 'xline'), may hold values from -6 to 6
Outputs:
- values: float32 [2, 131072], P(None, ('inline', 'xline'))
All inputs are finite; a program needn't handle non-finite values.
Results may differ from a plain program's by a relative error of at most 0.0003.
Values sent between devices are 32-bit elements; how exact they have to be, the bound alone decides.
No kernel may reach another device: no remote copies, remote signals or barrier semaphores. Data moves between devices by JAX's collectives and lax.ppermute only.
A program may use at most 64 MiB of HBM per device.

v0:
```python
import math

import jax
import jax.numpy as jnp
import numpy as np
from jax import lax
from jax.experimental import pallas as pl
from jax.experimental.pallas import tpu as pltpu
from jax.sharding import PartitionSpec as P

NF = 256
COLS = 256
GC = 4
N_INLINE = 32
N_XLINE = 16
KAPPA = 40.0
AXES = ("inline", "xline")
F32 = jnp.float32
BF16 = jnp.bfloat16

NODES = 0.5 * np.cos(np.arange(5) * (math.pi / 4.0))


def basis_at(points):
    rows = []
    for k in range(5):
        factor = np.ones_like(points)
        for j in range(5):
            if j != k:
                factor = factor * (points - NODES[j]) / (NODES[k] - NODES[j])
        rows.append(factor)
    return np.stack(rows)


CHILD = [basis_at((t - 0.5) * 0.5 + 0.5 * NODES) for t in (0, 1)]
LEAF_INLINE = basis_at(np.array([0.0]))[:, 0]
LEAF_XLINE = basis_at((np.arange(GC) + 0.5) / GC - 0.5)


def gather_groups():
    groups = []
    for base in range(N_INLINE * N_XLINE):
        a, b = base // N_XLINE, base % N_XLINE
        if a & 3 or b & 3:
            continue
        members = []
        for j in range(16):
            a0, b0, a1, b1 = j >> 3 & 1, j >> 2 & 1, j >> 1 & 1, j & 1
            members.append((a | a0 | a1 << 1) * N_XLINE + (b | b0 | b1 << 1))
        groups.append(members)
    return groups


def scatter_groups():
    groups = []
    for base in range(N_INLINE * N_XLINE):
        a, b = base // N_XLINE, base % N_XLINE
        if a >> 2 or b >> 2:
            continue
        members = []
        for j in range(32):
            k6, k7, k5, k3, k4 = j >> 4 & 1, j >> 3 & 1, j >> 2 & 1, j >> 1 & 1, j & 1
            members.append(
                (a | k3 << 2 | k5 << 3 | k7 << 4) * N_XLINE + (b | k4 << 2 | k6 << 3)
            )
        groups.append(members)
    return groups


def series(scale, bound, odd):
    coefs = []
    n = 0
    while True:
        power = 2 * n + (1 if odd else 0)
        size = (scale * bound) ** power / math.factorial(power)
        if size < 1e-8:
            return coefs
        coefs.append((-1.0) ** n * scale**power / math.factorial(power))
        n += 1


def poly(coefs, square):
    total = square * coefs[-1] + coefs[-2]
    for coef in coefs[-3::-1]:
        total = total * square + coef
    return total


def sincos_small(r, scale, bound):
    square = r * r
    return r * poly(series(scale, bound, True), square), poly(series(scale, bound, False), square)


def sincos_wide(x):
    turns = jnp.floor(x * (2.0 / math.pi) + 0.5)
    r = x - turns * 1.5703125
    r = r - turns * 4.837512969970703125e-4
    r = r - turns * 7.54978995489188216e-8
    sine, cosine = sincos_small(r, 1.0, 0.8)
    quarter = turns.astype(jnp.int32)
    swap = (quarter & 1) == 1
    s = jnp.where(swap, cosine, sine)
    c = jnp.where(swap, sine, cosine)
    s = jnp.where((quarter & 2) == 2, -s, s)
    c = jnp.where(((quarter + 1) & 2) == 2, -c, c)
    return s, c


def cmul(ar, ai, br, bi):
    return ar * br - ai * bi, ar * bi + ai * br


def full(value):
    return jnp.full((8, 128), value, F32)


def kernel(where_ref, rows_ref, out_ref, v_ref, tab_ref, leaf_ref, p_ref, q_ref, wa_ref, wb_ref, x_ref):
    a = where_ref[0]
    b = where_ref[1]
    lane = lax.broadcasted_iota(jnp.int32, (8, 128), 1)
    sub = lax.broadcasted_iota(jnp.int32, (8, 128), 0)
    bit2 = sub >> 2 & 1
    bit1 = sub >> 1 & 1
    bit0 = sub & 1

    left = lax.broadcasted_iota(jnp.int32, (16, 8, 128), 2) < 64
    re = rows_ref[:, 0:8, :]
    im = rows_ref[:, 8:16, :]
    re_r = pltpu.roll(re, 64, 2)
    im_r = pltpu.roll(im, 64, 2)
    v_ref[0, 0] = jnp.where(left, re, -im_r)
    v_ref[1, 0] = jnp.where(left, re_r, -im)
    v_ref[0, 1] = jnp.where(left, im, re_r)
    v_ref[1, 1] = jnp.where(left, im_r, re)

    column = lane + ((a & 1) << 7)

    def digits(places):
        coord = full(0.5 * 0.5 ** len(places))
        for rank, place in enumerate(places):
            coord = coord + (column >> place & 1).astype(F32) * 0.5 ** (rank + 1)
        return coord

    g0 = digits((7, 4, 1))
    g1 = digits((6, 3, 0))
    g2 = digits((5, 2))

    def sign_of(bit):
        return (2 * bit - 1).astype(F32)

    a_base = a & ~3
    b_base = b & ~3

    for half in range(2):
        box_a = (a_base + half + 2 * bit1).astype(F32)
        box_b = (b_base + bit2 + 2 * bit0).astype(F32)
        x0 = (box_a + 0.5) * (1.0 / N_INLINE)
        part = (0.5 + g0) * (0.5 + g0) + g1 * (x0 * x0)
        for c in range(GC):
            at = pl.ds(c * 16 + half * 8, 8)
            x1 = (box_b + (c + 0.5) / GC) * (1.0 / N_XLINE)
            radicand = part + g2 * (x1 * x1)
            step = (KAPPA / NF) * jnp.sqrt(radicand)
            tab_ref[0, at, :] = step
            s, co = sincos_wide(step * 132.0)
            s64, c64 = sincos_wide(step * 64.0)
            for f1 in range(4):
                tab_ref[1 + 2 * f1, at, :] = co
                tab_ref[2 + 2 * f1, at, :] = s
                if f1 < 3:
                    co, s = cmul(co, s, c64, s64)
            s8, c8 = sincos_wide(step * 8.0)
            co, s = c8, s8
            for f2 in range(1, 8):
                tab_ref[7 + 2 * f2, at, :] = co
                tab_ref[8 + 2 * f2, at, :] = s
                if f2 < 7:
                    co, s = cmul(co, s, c8, s8)

    basis = []
    for f1 in range(4):
        z = ((lane & 63).astype(F32) + (f1 * 64 + 0.5)) * (1.0 / NF) - 0.5
        factor = jnp.zeros((8, 128), F32)
        for k in range(5):
            scale = 1.0
            for j in range(5):
                if j != k:
                    scale = scale / (NODES[k] - NODES[j])
            factor = jnp.where(sub == k, scale, factor)
        for j in range(5):
            factor = factor * jnp.where(sub == j, 1.0, z - NODES[j])
        basis.append(factor)

    offset = sub.astype(F32) - 3.5

    def leaf_box(box, carry):
        totals = []
        for c in range(GC):
            row = c * 16 + box

            def table(i):
                return jnp.broadcast_to(tab_ref[i, pl.ds(row, 1), :], (8, 128))

            s_a, c_a = sincos_small(table(0) * offset, 1.0, 1.15)
            cos_rows, sin_rows = [c_a], [s_a]
            for f2 in range(1, 8):
                cr, sr = cmul(c_a, s_a, table(7 + 2 * f2), table(8 + 2 * f2))
                cos_rows.append(cr)
                sin_rows.append(sr)
            right = jnp.concatenate(cos_rows + sin_rows, axis=0)
            right_hi = right.astype(BF16)
            right_lo = (right - right_hi.astype(F32)).astype(BF16)
            rows = []
            for f1 in range(4):
                for part in range(2):
                    sample = v_ref[f1 & 1, part, pl.ds(box, 1), 2 * c + f1 // 2, :]
                    rows.append(basis[f1] * jnp.broadcast_to(sample, (8, 128)))
            lhs = jnp.concatenate(rows, axis=0)
            lhs_hi = lhs.astype(BF16)
            lhs_lo = (lhs - lhs_hi.astype(F32)).astype(BF16)
            both = jnp.concatenate([lhs_hi, lhs_hi], axis=1)
            mixed = jnp.dot(both, jnp.concatenate([right_hi, right_lo], axis=0), preferred_element_type=F32)
            mixed = mixed + jnp.dot(lhs_lo, right_hi, preferred_element_type=F32)
            t_re = None
            for f1 in range(4):
                u_re = mixed[f1 * 16 : f1 * 16 + 8]
                u_im = mixed[f1 * 16 + 8 : f1 * 16 + 16]
                r_re, r_im = cmul(u_re, u_im, table(1 + 2 * f1), table(2 + 2 * f1))
                t_re, t_im = (r_re, r_im) if t_re is None else (t_re + r_re, t_im + r_im)
            totals.append((t_re, t_im))
        for a1 in range(5):
            for part in range(2):
                total = totals[0][part] * float(LEAF_XLINE[a1, 0])
                for c in range(1, GC):
                    total = total + totals[c][part] * float(LEAF_XLINE[a1, c])
                leaf_ref[pl.ds((a1 * 16 + part) * 16 + box, 8, stride=32), :] = total
        return carry

    lax.fori_loop(0, 16, leaf_box, 0)

    def squares(low, width):
        return [(low + width * (float(NODES[k]) + 0.5)) * (low + width * (float(NODES[k]) + 0.5)) for k in range(5)]

    def prepare(low0, width0, low1, width1, slot=0):
        x0 = squares(low0, width0)
        x1 = squares(low1, width1)
        for k in range(5):
            p_ref[slot, k] = full(0.0) + x0[k]
            q_ref[slot, k] = full(0.0) + x1[k]

    def factors(anchor_sq, centre, slot, b0, b1, dim, move, bound):
        xx0 = p_ref[slot, b0]
        xx1 = q_ref[slot, b1]
        radicand = anchor_sq + centre[1] * xx0 + centre[2] * xx1
        root = radicand * lax.rsqrt(radicand)
        result = []
        for sigma in move:
            if dim == 0:
                moved = radicand + sigma
            elif dim == 1:
                moved = radicand + sigma * xx0
            else:
                moved = radicand + sigma * xx1
            change = moved * lax.rsqrt(moved) - root
            s_u, c_u = sincos_small(change, 0.5 * KAPPA, bound)
            s_v, c_v = sincos_small(change, KAPPA * float(NODES[1]), bound)
            result.append((c_u, s_u, c_v, s_v))
        return result

    def five(factor):
        c1, s1, cv, sv = factor
        c2 = c1 * c1 - s1 * s1
        s2 = c1 * s1
        s2 = s2 + s2
        c3, s3 = cmul(c2, s2, c1, s1)
        cc, ss, cs, sc = c2 * cv, s2 * sv, c2 * sv, s2 * cv
        return [(c3, s3), (cc - ss, sc + cs), (c2, s2), (cc + ss, sc - cs), (c1, s1)]

    def moves(centre, dim, q, sigmas):
        if dim == 0:
            return [2.0 * q * sigma * (0.5 + centre[0]) + q * q for sigma in sigmas]
        return [q * sigma + full(0.0) for sigma in sigmas]

    def merge(axis, dim, q, sides, centre, sigmas, read, write, combine):
        anchor = 0.5 + centre[0]
        anchor_sq = anchor * anchor
        step = moves(centre, dim, q, sigmas)

        def body(other, carry):
            for m in range(len(sigmas)):
                pass
            for side, (slot, coef) in enumerate(sides):
                for b in range(5):
                    b0, b1 = (b, other) if axis == 0 else (other, b)
                    made = factors(anchor_sq, centre, slot, b0, b1, dim, step, q)
                    turns = [five(item) for item in made]
                    for b2 in range(5):
                        w_re, w_im = read(side, b0, b1, b2)
                        for m in range(len(sigmas)):
                            x_re, x_im = cmul(w_re, w_im, turns[m][b2][0], turns[m][b2][1])
                            at = ((m * 2 + side) * 5 + b) * 10 + b2 * 2
                            x_ref[at] = x_re
                            x_ref[at + 1] = x_im
            for m in range(len(sigmas)):
                for comp in range(10):
                    for i in range(5):
                        total = None
                        for side, (slot, coef) in enumerate(sides):
                            for b in range(5):
                                item = x_ref[((m * 2 + side) * 5 + b) * 10 + comp] * coef(i, b)
                                total = item if total is None else total + item
                        i0, i1 = (i, other) if axis == 0 else (other, i)
                        write(m, i0, i1, comp, combine(total))
            return carry

        lax.fori_loop(0, 5, body, 0)

    def chosen(mask):
        table = [
            [jnp.where(mask, float(CHILD[1][i, j]), float(CHILD[0][i, j])) for j in range(5)]
            for i in range(5)
        ]
        return lambda i, j: table[i][j]

    def state_reader(ref, index):
        def read(side, b0, b1, b2):
            at = (b0 * 5 + b1) * 10 + b2 * 2
            return ref[index, at], ref[index, at + 1]

        return read

    def state_writer(ref, index_of):
        def write(m, i0, i1, comp, value):
            ref[index_of(m), (i0 * 5 + i1) * 10 + comp] = value

        return write

    unit_b = (b_base + bit2 + 2 * bit0).astype(F32) * (1.0 / N_XLINE)
    unit_a = (a_base + 2 * bit1).astype(F32) * (1.0 / N_INLINE)
    prepare(unit_a, 1.0 / N_INLINE, unit_b, 1.0 / N_XLINE, 0)
    prepare(unit_a + 1.0 / N_INLINE, 1.0 / N_INLINE, unit_b, 1.0 / N_XLINE, 1)

    def leaf_read(side, b0, b1, b2):
        base = (b1 * 8 + b2) * 32 + side * 8
        if not isinstance(base, int):
            base = pl.multiple_of(base, 8)
        return leaf_ref[pl.ds(base, 8), :], leaf_ref[pl.ds(base + 16, 8), :]

    merge(
        0, 2, 2.0**-4,
        [
            (t, (lambda t: lambda i, j: float(CHILD[t][i, j] * LEAF_INLINE[j]))(t))
            for t in (0, 1)
        ],
        (g0, g1, g2), [sign_of(full(0).astype(jnp.int32) + (b & 1))],
        leaf_read, state_writer(wa_ref, lambda m: 0), lambda v: v,
    )
    g2 = g2 + sign_of(b & 1) * 2.0**-4

    prepare(unit_a, 2.0 / N_INLINE, unit_b, 1.0 / N_XLINE)
    merge(
        1, 0, 2.0**-5, [(0, chosen(bit2 == 1))], (g0, g1, g2),
        [sign_of(full(0).astype(jnp.int32) + (a >> 1 & 1))],
        state_reader(wa_ref, 0), state_writer(wb_ref, lambda m: 0),
        lambda v: v + pltpu.roll(v, 4, 0),
    )
    g0 = g0 + sign_of(a >> 1 & 1) * 2.0**-5

    low_b = (b_base + 2 * bit0).astype(F32) * (1.0 / N_XLINE)
    prepare(unit_a, 2.0 / N_INLINE, low_b, 2.0 / N_XLINE)
    merge(
        0, 1, 2.0**-5, [(0, chosen(bit1 == 1))], (g0, g1, g2),
        [sign_of(full(0).astype(jnp.int32) + (b >> 1 & 1))],
        state_reader(wb_ref, 0), state_writer(wa_ref, lambda m: 0),
        lambda v: v + pltpu.roll(v, 2, 0),
    )
    g1 = g1 + sign_of(b >> 1 & 1) * 2.0**-5

    node_a = full(0.0) + a_base.astype(F32) * (1.0 / N_INLINE)
    prepare(node_a, 4.0 / N_INLINE, low_b, 2.0 / N_XLINE)
    even = bit0 == 0
    merge(
        1, 2, 2.0**-5, [(0, chosen(bit0 == 1))], (g0, g1, g2), [sign_of(bit1)],
        state_reader(wa_ref, 0), state_writer(wb_ref, lambda m: 0),
        lambda v: v + jnp.where(even, pltpu.roll(v, 7, 0), pltpu.roll(v, 1, 0)),
    )
    g2 = g2 + sign_of(bit1) * 2.0**-5

    node_b = full(0.0) + b_base.astype(F32) * (1.0 / N_XLINE)
    none = full(0).astype(jnp.int32)
    prepare(node_a, 4.0 / N_INLINE, node_b, 4.0 / N_XLINE)
    merge(
        0, 0, 2.0**-6, [(0, chosen(none + (a >> 2 & 1) == 1))], (g0, g1, g2), [sign_of(bit0)],
        state_reader(wb_ref, 0), state_writer(wa_ref, lambda m: 0), lambda v: v,
    )
    g0 = g0 + sign_of(bit0) * 2.0**-6

    node_a = full(0.0) + (a & ~7).astype(F32) * (1.0 / N_INLINE)
    prepare(node_a, 8.0 / N_INLINE, node_b, 4.0 / N_XLINE)
    merge(
        1, 1, 2.0**-6, [(0, chosen(none + (b >> 2 & 1) == 1))], (g0, g1, g2), [sign_of(bit2)],
        state_reader(wa_ref, 0), state_writer(wb_ref, lambda m: 0), lambda v: v,
    )
    g1 = g1 + sign_of(bit2) * 2.0**-6

    node_b = full(0.0) + (b & ~7).astype(F32) * (1.0 / N_XLINE)
    prepare(node_a, 8.0 / N_INLINE, node_b, 8.0 / N_XLINE)
    merge(
        0, 2, 2.0**-6, [(0, chosen(none + (a >> 3 & 1) == 1))], (g0, g1, g2), [-1.0, 1.0],
        state_reader(wb_ref, 0), state_writer(wa_ref, lambda m: m), lambda v: v,
    )

    node_a = full(0.0) + (a & ~15).astype(F32) * (1.0 / N_INLINE)
    prepare(node_a, 16.0 / N_INLINE, node_b, 8.0 / N_XLINE)
    mask = none + (b >> 3 & 1) == 1
    for k6 in range(2):
        merge(
            1, 0, 2.0**-7, [(0, chosen(mask))],
            (g0, g1, g2 + (2 * k6 - 1) * 2.0**-6), [-1.0, 1.0],
            state_reader(wa_ref, k6),
            (lambda k6: state_writer(wb_ref, lambda m: 2 * k6 + m))(k6), lambda v: v,
        )

    prepare(node_a, 16.0 / N_INLINE, full(0.0), 16.0 / N_XLINE)
    scale = 1.0 / math.sqrt(GC * NF * N_INLINE * N_XLINE)
    for k6 in range(2):
        for k7 in range(2):
            centre = (g0 + (2 * k7 - 1) * 2.0**-7, g1, g2 + (2 * k6 - 1) * 2.0**-6)
            anchor = 0.5 + centre[0]
            anchor_sq = anchor * anchor
            step = moves(centre, 1, 2.0**-7, [-1.0, 1.0])
            read = state_reader(wb_ref, 2 * k6 + k7)

            def body(b0, sums, anchor_sq=anchor_sq, centre=centre, step=step, read=read):
                sums = list(sums)
                for b1 in range(5):
                    w = [read(0, b0, b1, b2) for b2 in range(5)]
                    wp_re, wp_im = w[1][0] + w[3][0], w[1][1] + w[3][1]
                    wm_re, wm_im = w[1][0] - w[3][0], w[1][1] - w[3][1]
                    made = factors(anchor_sq, centre, 0, b0, b1, 1, step, 2.0**-7)
                    for m, (cu, su, cv, sv) in enumerate(made):
                        t_re, t_im = cmul(w[0][0], w[0][1], cu, su)
                        t_re = t_re + (w[2][0] + (cv * wp_re - sv * wm_im))
                        t_im = t_im + (w[2][1] + (cv * wp_im + sv * wm_re))
                        t_re, t_im = cmul(t_re, t_im, cu, su)
                        t_re, t_im = cmul(t_re + w[4][0], t_im + w[4][1], cu, su)
                        sums[2 * m] = sums[2 * m] + t_re
                        sums[2 * m + 1] = sums[2 * m + 1] + t_im
                return tuple(sums)

            sums = lax.fori_loop(0, 5, body, tuple(full(0.0) for _ in range(4)))
            for m in range(2):
                for part in range(2):
                    out_ref[pl.ds((2 * k6 + k7) * 32 + part * 2 + m, 8, stride=4), :] = (
                        sums[2 * m + part] * scale
                    )


def contributions(where, rows, interpret=False):
    return pl.pallas_call(
        kernel,
        out_shape=jax.ShapeDtypeStruct((128, 128), F32),
        in_specs=[
            pl.BlockSpec(memory_space=pltpu.SMEM),
            pl.BlockSpec(memory_space=pltpu.VMEM),
        ],
        out_specs=pl.BlockSpec(memory_space=pltpu.VMEM),
        scratch_shapes=[
            pltpu.VMEM((2, 2, 16, 8, 128), F32),
            pltpu.VMEM((23, 64, 128), F32),
            pltpu.VMEM((1280, 128), F32),
            pltpu.VMEM((2, 5, 8, 128), F32),
            pltpu.VMEM((2, 5, 8, 128), F32),
            pltpu.VMEM((2, 250, 8, 128), F32),
            pltpu.VMEM((4, 250, 8, 128), F32),
            pltpu.VMEM((200, 8, 128), F32),
        ],
        interpret=interpret,
    )(where, rows)


def shards(samples):
    rows = samples.reshape(1, 16, 128)
    rows = jnp.broadcast_to(rows, (16, 16, 128))
    rows = lax.all_to_all(rows, AXES, 0, 0, axis_index_groups=gather_groups())
    where = jnp.stack([lax.axis_index("inline"), lax.axis_index("xline")]).astype(jnp.int32)
    parts = contributions(where, rows).reshape(32, 4, 128)
    parts = lax.all_to_all(parts, AXES, 0, 0, axis_index_groups=scatter_groups())
    return jnp.sum(parts, axis=0).reshape(2, COLS)


def solution(mesh):
    return jax.shard_map(
        shards,
        mesh=mesh,
        in_specs=(P(None, "inline", "xline"),),
        out_specs=P(None, AXES),
        check_vma=False,
    )
```

profile of v0, /device:TPU:1, one launch (start us, length us, event | category | flops | bytes accessed | tf_op | source)
XLA Modules:
  0.0 66.3 jit_solution(7896246132910675986)
XLA Ops:
  0.0 1.4 %broadcast_in_dim.8 = f32[16,16,128]{2,1,0:T(8,128)} broadcast(f32[16,128]{1,0:T(8,128)} %bitcast.5), dimensions={1,2} | broadcast | bytes 139264 | tf_op jit(solution)/shard_map/broadcast_in_dim | solution.py:484
  1.4 10.2 %all-to-all-start = ((f32[16,16,128]{2,1,0:T(8,128)}), f32[16,16,128]{2,1,0:T(8,128)S(1)}, u32[]{:S(2)}, u32[]{:S(2)}) async-start(f32[16,16,128]{2,1,0:T(8,128)} %broadcast_in_dim.8), calls=%async_computation | async-start | bytes 262144 | tf_op jit(solution)/shard_map/all_to_all | solution.py:485
  11.5 0.6 pad_add_fusion.where_ref
  12.1 6.7 %all-to-all-done.rows_ref = f32[16,16,128]{2,1,0:T(8,128)S(1)} async-done(((f32[16,16,128]{2,1,0:T(8,128)}), f32[16,16,128]{2,1,0:T(8,128)S(1)}, u32[]{:S(2)}, u32[]{:S(2)}) %all-to-all-start) | async-done | bytes 131104 | tf_op jit(solution)/shard_map/all_to_all | solution.py:485
  18.8 0.0 copy-start
  18.8 0.6 copy-done
  19.5 16.6 %shard_map.17 = f32[128,128]{1,0:T(8,128)} custom-call(s32[2]{0:T(128)} %pad_add_fusion.where_ref, f32[16,16,128]{2,1,0:T(8,128)} %copy-done), custom_call_target="tpu_custom_call" | custom-call | tf_op jit(solution)/shard_map/pallas_call | solution.py:460
  36.1 29.6 %all_to_all.10 = f32[32,4,128]{2,1,0:T(4,128)S(1)} all-to-all(f32[32,4,128]{2,1,0:T(4,128)} %bitcast.4), channel_id=1, replica_groups={{0,4,64,68,128,132,192,196,256,260,320,324,384,388,448,452,8,12,72,76,1..., dimensions={0} | all-to-all | bytes 131072 | tf_op jit(solution)/shard_map/all_to_all | solution.py:488
  65.7 0.6 reshape.9
  (1 shorter events, 0.0 us)
Async XLA Ops:
  1.4 17.5 %all-to-all-start = ((f32[16,16,128]{2,1,0:T(8,128)}), f32[16,16,128]{2,1,0:T(8,128)S(1)}, u32[]{:S(2)}, u32[]{:S(2)}) async-start(f32[16,16,128]{2,1,0:T(8,128)} %broadcast_in_dim.8), calls=%async_computation | async-start | bytes 262144 | tf_op jit(solution)/shard_map/all_to_all | solution.py:485
  18.8 0.7 copy-start
where the time goes:
time: 66.6 us; the launch traced here: 66.3 us
  blocking collectives  29.6 us (44%)
  Pallas kernels  16.6 us (25%)
  starting transfers between devices  10.2 us (15%)
  waiting for transfers between devices  6.71 us (10%)
  local copies, waits for them, and re-layouts  2.6 us (4%)
    all_to_all x1, blocking collectives, shards(): lax.all_to_all(parts, AXES, 0, 0, axis_index_groups=scatter_groups())  29.6 us
    pallas_call x1, Pallas kernels, contributions(): pl.pallas_call(kernel, out_shape=jax.ShapeDtypeStruct((128, 128), F32), i...  16.6 us
    all_to_all x1, starting transfers between devices, shards(): rows = lax.all_to_all(rows, AXES, 0, 0, axis_index_groups=gather_groups())  10.2 us
    all_to_all x1, waiting for transfers between devices, shards(): rows = lax.all_to_all(rows, AXES, 0, 0, axis_index_groups=gather_groups())  6.71 us
    broadcast_in_dim x1, local copies, waits for them, and re-layouts, shards(): rows = jnp.broadcast_to(rows, (16, 16, 128))  1.36 us
  transfers between devices with their start and end apart: 1, of which 1 were waited for; matrix products, arithmetic and copies ran while one was open for 1% of the time, Pallas kernels for 0%

commit v1 on v0

v1 whole, which is shorter than its diff:
```python
import math

import jax
import jax.numpy as jnp
import numpy as np
from jax import lax
from jax.experimental import pallas as pl
from jax.experimental.pallas import tpu as pltpu
from jax.sharding import PartitionSpec as P

NF = 256
COLS = 256
GC = 4
N_INLINE = 32
N_XLINE = 16
KAPPA = 40.0
AXES = ("inline", "xline")
F32 = jnp.float32
BF16 = jnp.bfloat16

ROOT = math.sqrt(0.5)
NODES = 0.5 * np.array([1.0, ROOT, 0.0, -ROOT, -1.0])


def basis_at(points):
    rows = []
    for k in range(5):
        factor = np.ones_like(points)
        for j in range(5):
            if j != k:
                factor = factor * (points - NODES[j]) / (NODES[k] - NODES[j])
        rows.append(factor)
    return np.stack(rows)


CHILD = [basis_at((t - 0.5) * 0.5 + 0.5 * NODES) for t in (0, 1)]
LEAF_XLINE = basis_at((np.arange(GC) + 0.5) / GC - 0.5)


def gather_groups():
    groups = []
    for base in range(N_INLINE * N_XLINE):
        a, b = base // N_XLINE, base % N_XLINE
        if a & 3 or b & 3:
            continue
        members = []
        for j in range(16):
            a0, b0, a1, b1 = j >> 3 & 1, j >> 2 & 1, j >> 1 & 1, j & 1
            members.append((a | a0 | a1 << 1) * N_XLINE + (b | b0 | b1 << 1))
        groups.append(members)
    return groups


def scatter_groups():
    groups = []
    for base in range(N_INLINE * N_XLINE):
        a, b = base // N_XLINE, base % N_XLINE
        if a >> 2 or b >> 2:
            continue
        members = []
        for j in range(32):
            k6, k7, k5, k3, k4 = j >> 4 & 1, j >> 3 & 1, j >> 2 & 1, j >> 1 & 1, j & 1
            members.append(
                (a | k3 << 2 | k5 << 3 | k7 << 4) * N_XLINE + (b | k4 << 2 | k6 << 3)
            )
        groups.append(members)
    return groups


def series(scale, bound, odd):
    coefs = []
    n = 0
    while True:
        power = 2 * n + (1 if odd else 0)
        size = (scale * bound) ** power / math.factorial(power)
        if size < 1e-8:
            return coefs
        coefs.append((-1.0) ** n * scale**power / math.factorial(power))
        n += 1


def poly(coefs, square):
    total = square * coefs[-1] + coefs[-2]
    for coef in coefs[-3::-1]:
        total = total * square + coef
    return total


def sincos_small(r, scale, bound):
    square = r * r
    return r * poly(series(scale, bound, True), square), poly(series(scale, bound, False), square)


def sincos_wide(x):
    turns = jnp.floor(x * (2.0 / math.pi) + 0.5)
    r = x - turns * 1.5703125
    r = r - turns * 4.837512969970703125e-4
    r = r - turns * 7.54978995489188216e-8
    sine, cosine = sincos_small(r, 1.0, 0.8)
    quarter = turns.astype(jnp.int32)
    swap = (quarter & 1) == 1
    s = jnp.where(swap, cosine, sine)
    c = jnp.where(swap, sine, cosine)
    s = jnp.where((quarter & 2) == 2, -s, s)
    c = jnp.where(((quarter + 1) & 2) == 2, -c, c)
    return s, c


def cmul(ar, ai, br, bi):
    return ar * br - ai * bi, ar * bi + ai * br


def full(value):
    return jnp.full((8, 128), value, F32)


def spot(bit):
    return (2 * bit - 1).astype(F32)


def places(where_ref):
    a = where_ref[0]
    b = where_ref[1]
    lane = lax.broadcasted_iota(jnp.int32, (8, 128), 1)
    sub = lax.broadcasted_iota(jnp.int32, (8, 128), 0)
    column = lane + ((a & 1) << 7)

    def digits(where):
        coord = full(0.5 * 0.5 ** len(where))
        for rank, place in enumerate(where):
            coord = coord + (column >> place & 1).astype(F32) * 0.5 ** (rank + 1)
        return coord

    return a, b, lane, sub, (digits((7, 4, 1)), digits((6, 3, 0)), digits((5, 2)))


def five(factor):
    c1, s1, cv, sv = factor
    c2 = c1 * c1 - s1 * s1
    s2 = c1 * s1
    s2 = s2 + s2
    c3, s3 = cmul(c2, s2, c1, s1)
    cc, ss, cs, sc = c2 * cv, s2 * sv, c2 * sv, s2 * cv
    return [(c3, s3), (cc - ss, sc + cs), (c2, s2), (cc + ss, sc - cs), (c1, s1)]


SETS = ((0, 1), (1, 2), (2, 3), (3, 4), (4, 5), (5, 7), (7, 11), (11, 19))
TURN = 40
NEAR = 11


def stretch(k, source, target, sem):
    low, high = SETS[k]
    at = pl.ds(low * 100, (high - low) * 100)
    return pltpu.make_async_copy(source.at[at], target.at[at], sem)


def table_kernel(where_ref, near_ref, turn_ref, far_ref, table_ref, tab_ref, far_s, table_s, p_ref, q_ref, s_ref, sems):
    a, b, lane, sub, (g0, g1, g2) = places(where_ref)
    bit2 = sub >> 2 & 1
    bit1 = sub >> 1 & 1
    bit0 = sub & 1
    none = sub * 0
    a_base = a & ~3
    b_base = b & ~3

    for half in range(2):
        box_a = (a_base + half + 2 * bit1).astype(F32)
        box_b = (b_base + bit2 + 2 * bit0).astype(F32)
        x0 = (box_a + 0.5) * (1.0 / N_INLINE)
        part = (0.5 + g0) * (0.5 + g0) + g1 * (x0 * x0)
        for c in range(GC):
            at = pl.ds(c * 16 + half * 8, 8)
            x1 = (box_b + (c + 0.5) / GC) * (1.0 / N_XLINE)
            radicand = part + g2 * (x1 * x1)
            step = (KAPPA / NF) * (radicand * lax.rsqrt(radicand))
            tab_ref[0, at, :] = step
            s, co = sincos_wide(step * 132.0)
            s64, c64 = sincos_wide(step * 64.0)
            for f1 in range(4):
                turn_ref[TURN + f1 * 16 + c * 2 + half] = co
                turn_ref[TURN + f1 * 16 + 8 + c * 2 + half] = s
                if f1 < 3:
                    co, s = cmul(co, s, c64, s64)
            s8, c8 = sincos_wide(step * 8.0)
            co, s = c8, s8
            for f2 in range(1, 8):
                tab_ref[2 * f2 - 1, at, :] = co
                tab_ref[2 * f2, at, :] = s
                if f2 < 7:
                    co, s = cmul(co, s, c8, s8)

    offset = sub.astype(F32) - 3.5

    def wave(box, ref, first):
        for c in range(GC):
            row = c * 16 + box

            def table(i):
                return jnp.broadcast_to(tab_ref[i, pl.ds(row, 1), :], (8, 128))

            s_a, c_a = sincos_small(table(0) * offset, 1.0, 1.15)
            cos_rows, sin_rows = [c_a], [s_a]
            for f2 in range(1, 8):
                cr, sr = cmul(c_a, s_a, table(2 * f2 - 1), table(2 * f2))
                cos_rows.append(cr)
                sin_rows.append(sr)
            right = jnp.concatenate(cos_rows + sin_rows, axis=0)
            right_hi = right.astype(BF16)
            ref[(box - first) * GC + c, 0:128, :] = right_hi
            ref[(box - first) * GC + c, 128:256, :] = (right - right_hi.astype(F32)).astype(BF16)

    def far_wave(box, carry):
        wave(box, far_s, NEAR)
        return carry

    def near_wave(box, carry):
        wave(box, near_ref, 0)
        return carry

    lax.fori_loop(NEAR, 16, far_wave, 0)
    save_far = pltpu.make_async_copy(far_s, far_ref, sems.at[8])
    save_far.start()

    def save(k):
        stretch(k, table_s, table_ref, sems.at[k]).start()

    def box_squares(low, width):
        return [(low + width * (float(NODES[k]) + 0.5)) * (low + width * (float(NODES[k]) + 0.5)) for k in range(5)]

    def level(low0, width0, low1, width1, centre, dim, q, sigmas, store, first=False):
        anchor = 0.5 + centre[0]
        x0 = box_squares(low0, width0)
        x1 = box_squares(low1, width1)
        for k in range(5):
            p_ref[k] = anchor * anchor + centre[1] * x0[k]
            q_ref[k] = centre[2] * x1[k]
            if dim:
                s_ref[k] = (x0 if dim == 1 else x1)[k] * q + full(0.0)
        if dim == 0:
            gaps = [2.0 * q * sigma * anchor + q * q for sigma in sigmas]

        def body(b1, carry):
            across = q_ref[b1]
            for b0 in (2,) if first else range(5):
                radicand = p_ref[b0] + across
                root = radicand * lax.rsqrt(radicand)
                for m, sigma in enumerate(sigmas):
                    if dim == 0:
                        moved = radicand + gaps[m]
                    else:
                        gap = s_ref[b0 if dim == 1 else b1]
                        if isinstance(sigma, float):
                            moved = radicand + gap if sigma > 0 else radicand - gap
                        else:
                            moved = radicand + sigma * gap
                    change = moved * lax.rsqrt(moved) - root
                    s_u, c_u = sincos_small(change, 0.5 * KAPPA, q)
                    s_v, c_v = sincos_small(change, KAPPA * float(NODES[1]), q)
                    store(m, b0, b1, (c_u, s_u, c_v, s_v))
            return carry

        lax.fori_loop(0, 5, body, 0)

    def into_levels(index_of):
        def store(m, b0, b1, factor):
            for k in range(4):
                table_s[index_of(m) * 100 + (b0 * 5 + b1) * 4 + k] = factor[k]

        return store

    unit_b = (b_base + bit2 + 2 * bit0).astype(F32) * (1.0 / N_XLINE)
    unit_a = (a_base + 2 * bit1).astype(F32) * (1.0 / N_INLINE)
    for side in range(2):

        def into_first(m, b0, b1, factor, side=side):
            for k in range(4):
                turn_ref[side * 20 + b1 * 4 + k] = factor[k]

        level(
            unit_a + side / N_INLINE, 1.0 / N_INLINE, unit_b, 1.0 / N_XLINE,
            (g0, g1, g2), 2, 2.0**-4, [spot(none + (b & 1))], into_first, True,
        )
    g2 = g2 + spot(none + (b & 1)) * 2.0**-4

    level(
        unit_a, 2.0 / N_INLINE, unit_b, 1.0 / N_XLINE,
        (g0, g1, g2), 0, 2.0**-5, [spot(none + (a >> 1 & 1))], into_levels(lambda m: 0),
    )
    save(0)
    g0 = g0 + spot(none + (a >> 1 & 1)) * 2.0**-5

    low_b = (b_base + 2 * bit0).astype(F32) * (1.0 / N_XLINE)
    level(
        unit_a, 2.0 / N_INLINE, low_b, 2.0 / N_XLINE,
        (g0, g1, g2), 1, 2.0**-5, [spot(none + (b >> 1 & 1))], into_levels(lambda m: 1),
    )
    save(1)
    g1 = g1 + spot(none + (b >> 1 & 1)) * 2.0**-5

    node_a = full(0.0) + a_base.astype(F32) * (1.0 / N_INLINE)
    level(
        node_a, 4.0 / N_INLINE, low_b, 2.0 / N_XLINE,
        (g0, g1, g2), 2, 2.0**-5, [spot(bit1)], into_levels(lambda m: 2),
    )
    save(2)
    g2 = g2 + spot(bit1) * 2.0**-5

    node_b = full(0.0) + b_base.astype(F32) * (1.0 / N_XLINE)
    level(
        node_a, 4.0 / N_INLINE, node_b, 4.0 / N_XLINE,
        (g0, g1, g2), 0, 2.0**-6, [spot(bit0)], into_levels(lambda m: 3),
    )
    save(3)
    g0 = g0 + spot(bit0) * 2.0**-6

    node_a = full(0.0) + (a & ~7).astype(F32) * (1.0 / N_INLINE)
    level(
        node_a, 8.0 / N_INLINE, node_b, 4.0 / N_XLINE,
        (g0, g1, g2), 1, 2.0**-6, [spot(bit2)], into_levels(lambda m: 4),
    )
    save(4)
    g1 = g1 + spot(bit2) * 2.0**-6

    node_b = full(0.0) + (b & ~7).astype(F32) * (1.0 / N_XLINE)
    level(
        node_a, 8.0 / N_INLINE, node_b, 8.0 / N_XLINE,
        (g0, g1, g2), 2, 2.0**-6, [-1.0, 1.0], into_levels(lambda m: 5 + m),
    )
    save(5)

    node_a = full(0.0) + (a & ~15).astype(F32) * (1.0 / N_INLINE)
    for k6 in range(2):
        level(
            node_a, 16.0 / N_INLINE, node_b, 8.0 / N_XLINE,
            (g0, g1, g2 + (2 * k6 - 1) * 2.0**-6), 0, 2.0**-7, [-1.0, 1.0],
            into_levels((lambda k6: lambda m: 7 + 2 * k6 + m)(k6)),
        )
    save(6)

    for k6 in range(2):
        for k7 in range(2):

            def into_last(m, b0, b1, factor, first=11 + 4 * k6 + 2 * k7):
                for k in range(4):
                    table_s[(first + m) * 100 + (b0 * 5 + b1) * 4 + k] = factor[k]

            level(
                node_a, 16.0 / N_INLINE, full(0.0), 16.0 / N_XLINE,
                (g0 + (2 * k7 - 1) * 2.0**-7, g1, g2 + (2 * k6 - 1) * 2.0**-6), 1, 2.0**-7,
                [-1.0, 1.0], into_last,
            )
    save(7)
    lax.fori_loop(0, NEAR, near_wave, 0)
    save_far.wait()
    for k in range(8):
        stretch(k, table_s, table_ref, sems.at[k]).wait()


def kernel(where_ref, rows_ref, near_ref, turn_ref, far_ref, table_ref, out_ref, v_ref, leaf_ref, wa_ref, wb_ref, x_ref, far_s, table_s, sems):
    load_far = pltpu.make_async_copy(far_ref, far_s, sems.at[8])
    load_far.start()
    loads = [stretch(k, table_ref, table_s, sems.at[k]) for k in range(8)]
    for load in loads:
        load.start()
    a, b, lane, sub, unused = places(where_ref)

    left = lax.broadcasted_iota(jnp.int32, (16, 8, 128), 2) < 64
    re = rows_ref[:, 0:8, :]
    im = rows_ref[:, 8:16, :]
    re_r = pltpu.roll(re, 64, 2)
    im_r = pltpu.roll(im, 64, 2)
    v_ref[0, 0] = jnp.where(left, re, -im_r)
    v_ref[1, 0] = jnp.where(left, re_r, -im)
    v_ref[0, 1] = jnp.where(left, im, re_r)
    v_ref[1, 1] = jnp.where(left, im_r, re)

    basis = []
    for f1 in range(4):
        z = ((lane & 63).astype(F32) + (f1 * 64 + 0.5)) * (1.0 / NF) - 0.5
        factor = jnp.zeros((8, 128), F32)
        for k in range(5):
            scale = 1.0
            for j in range(5):
                if j != k:
                    scale = scale / (NODES[k] - NODES[j])
            factor = jnp.where(sub == k, scale, factor)
        for j in range(5):
            factor = factor * jnp.where(sub == j, 1.0, z - NODES[j])
        basis.append(factor)

    def leaf_one(box):
        totals = []
        for c in range(GC):
            def table(i):
                return jnp.broadcast_to(turn_ref[TURN + i * 8 + c * 2 + box // 8, pl.ds(box % 8, 1), :], (8, 128))

            rows = []
            for f1 in range(4):
                for part in range(2):
                    sample = v_ref[f1 & 1, part, pl.ds(box, 1), 2 * c + f1 // 2, :]
                    rows.append(basis[f1] * jnp.broadcast_to(sample, (8, 128)))
            lhs = jnp.concatenate(rows, axis=0)
            lhs_hi = lhs.astype(BF16)
            lhs_lo = (lhs - lhs_hi.astype(F32)).astype(BF16)
            both = jnp.concatenate([lhs_hi, lhs_hi], axis=1)
            right = near_ref[box * GC + c] if box < NEAR else far_s[(box - NEAR) * GC + c]
            mixed = jnp.dot(both, right, preferred_element_type=F32)
            mixed = mixed + jnp.dot(lhs_lo, right[0:128], preferred_element_type=F32)
            t_re = None
            for f1 in range(4):
                u_re = mixed[f1 * 16 : f1 * 16 + 8]
                u_im = mixed[f1 * 16 + 8 : f1 * 16 + 16]
                r_re, r_im = cmul(u_re, u_im, table(2 * f1), table(2 * f1 + 1))
                t_re, t_im = (r_re, r_im) if t_re is None else (t_re + r_re, t_im + r_im)
            totals.append((t_re, t_im))
        for a1 in range(5):
            for part in range(2):
                total = totals[0][part] * float(LEAF_XLINE[a1, 0])
                for c in range(1, GC):
                    total = total + totals[c][part] * float(LEAF_XLINE[a1, c])
                leaf_ref[pl.ds((a1 * 16 + part) * 16 + box, 8, stride=32), :] = total

    for box in range(16):
        if box == NEAR:
            load_far.wait()
        leaf_one(box)

    def merge(axis, points, sets, read, turn, weight, write, combine):
        def body(other, carry):
            for n, (side, p) in enumerate(points):
                b0, b1 = (p, other) if axis == 0 else (other, p)
                turns = [five(turn(m, side, b0, b1)) for m in range(sets)]
                for b2 in range(5):
                    w_re, w_im = read(side, b0, b1, b2)
                    for m in range(sets):
                        x_re, x_im = cmul(w_re, w_im, *turns[m][b2])
                        x_ref[(m * 5 + n) * 10 + 2 * b2] = x_re
                        x_ref[(m * 5 + n) * 10 + 2 * b2 + 1] = x_im
            for m in range(sets):
                for comp in range(10):
                    items = [x_ref[(m * 5 + n) * 10 + comp] for n in range(len(points))]
                    for i in range(5):
                        total = None
                        for (side, p), item in zip(points, items):
                            coef = weight(i, side, p)
                            if coef is None:
                                continue
                            term = item if isinstance(coef, float) and coef == 1.0 else item * coef
                            total = term if total is None else total + term
                        i0, i1 = (i, other) if axis == 0 else (other, i)
                        write(m, i0, i1, comp, combine(total))
            return carry

        lax.fori_loop(0, 5, body, 0)

    def chosen(mask):
        table = [
            [
                None
                if CHILD[0][i, j] == 0.0 and CHILD[1][i, j] == 0.0
                else jnp.where(mask, float(CHILD[1][i, j]), float(CHILD[0][i, j]))
                for j in range(5)
            ]
            for i in range(5)
        ]
        return lambda i, side, j: table[i][j]

    def lower(i, side, j):
        return None if CHILD[0][i, j] == 0.0 else float(CHILD[0][i, j])

    def flipped(axis, bit):
        def order(i0, i1):
            if axis == 0:
                return i0 + bit * (4 - 2 * i0), i1
            return i0, i1 + bit * (4 - 2 * i1)

        return order

    def same(i0, i1):
        return i0, i1

    def reader(ref, index, order=same):
        def read(side, b0, b1, b2):
            b0, b1 = order(b0, b1)
            at = (b0 * 5 + b1) * 10 + b2 * 2
            return ref[index, at], ref[index, at + 1]

        return read

    def turner(index_of, order=same):
        def turn(m, side, b0, b1):
            b0, b1 = order(b0, b1)
            at = index_of(m) * 100 + (b0 * 5 + b1) * 4
            return [table_s[at + k] for k in range(4)]

        return turn

    def writer(ref, index_of, order=same):
        def write(m, i0, i1, comp, value):
            i0, i1 = order(i0, i1)
            ref[index_of(m), (i0 * 5 + i1) * 10 + comp] = value

        return write

    line = [(0, j) for j in range(5)]

    def leaf_read(side, b0, b1, b2):
        base = pl.multiple_of((b1 * 8 + b2) * 32 + side * 8, 8)
        return leaf_ref[pl.ds(base, 8), :], leaf_ref[pl.ds(base + 16, 8), :]

    merge(
        0, [(0, 2), (1, 2)], 1, leaf_read,
        lambda m, side, b0, b1: [turn_ref[side * 20 + b1 * 4 + k] for k in range(4)],
        lambda i, side, j: float(CHILD[side][i, j]),
        writer(wa_ref, lambda m: 0), lambda v: v,
    )
    loads[0].wait()
    merge(
        1, line, 1, reader(wa_ref, 0), turner(lambda m: 0), chosen((sub >> 2 & 1) == 1),
        writer(wb_ref, lambda m: 0), lambda v: v + pltpu.roll(v, 4, 0),
    )
    loads[1].wait()
    merge(
        0, line, 1, reader(wb_ref, 0), turner(lambda m: 1), chosen((sub >> 1 & 1) == 1),
        writer(wa_ref, lambda m: 0), lambda v: v + pltpu.roll(v, 2, 0),
    )
    loads[2].wait()
    even = (sub & 1) == 0
    merge(
        1, line, 1, reader(wa_ref, 0), turner(lambda m: 2), chosen((sub & 1) == 1),
        writer(wb_ref, lambda m: 0),
        lambda v: v + jnp.where(even, pltpu.roll(v, 7, 0), pltpu.roll(v, 1, 0)),
    )
    loads[3].wait()
    order = flipped(0, a >> 2 & 1)
    merge(
        0, line, 1, reader(wb_ref, 0, order), turner(lambda m: 3, order), lower,
        writer(wa_ref, lambda m: 0, order), lambda v: v,
    )
    loads[4].wait()
    order = flipped(1, b >> 2 & 1)
    merge(
        1, line, 1, reader(wa_ref, 0, order), turner(lambda m: 4, order), lower,
        writer(wb_ref, lambda m: 0, order), lambda v: v,
    )
    loads[5].wait()
    order = flipped(0, a >> 3 & 1)
    merge(
        0, line, 2, reader(wb_ref, 0, order), turner(lambda m: 5 + m, order), lower,
        writer(wa_ref, lambda m: m, order), lambda v: v,
    )
    loads[6].wait()
    order = flipped(1, b >> 3 & 1)
    for k6 in range(2):
        merge(
            1, line, 2, reader(wa_ref, k6, order),
            turner((lambda k6: lambda m: 7 + 2 * k6 + m)(k6), order), lower,
            writer(wb_ref, (lambda k6: lambda m: 2 * k6 + m)(k6), order), lambda v: v,
        )

    loads[7].wait()
    scale = 1.0 / math.sqrt(GC * NF * N_INLINE * N_XLINE)
    for k67 in range(4):
        read = reader(wb_ref, k67)

        def body(b0, sums, k67=k67, read=read):
            sums = list(sums)
            for b1 in range(5):
                w = [read(0, b0, b1, b2) for b2 in range(5)]
                wp_re, wp_im = w[1][0] + w[3][0], w[1][1] + w[3][1]
                wm_re, wm_im = w[1][0] - w[3][0], w[1][1] - w[3][1]
                for m in range(2):
                    cu, su, cv, sv = (table_s[(11 + 2 * k67 + m) * 100 + (b0 * 5 + b1) * 4 + k] for k in range(4))
                    t_re, t_im = cmul(w[0][0], w[0][1], cu, su)
                    t_re = t_re + (w[2][0] + (cv * wp_re - sv * wm_im))
                    t_im = t_im + (w[2][1] + (cv * wp_im + sv * wm_re))
                    t_re, t_im = cmul(t_re, t_im, cu, su)
                    t_re, t_im = cmul(t_re + w[4][0], t_im + w[4][1], cu, su)
                    sums[2 * m] = sums[2 * m] + t_re
                    sums[2 * m + 1] = sums[2 * m + 1] + t_im
            return tuple(sums)

        sums = lax.fori_loop(0, 5, body, tuple(full(0.0) for _ in range(4)))
        for m in range(2):
            for part in range(2):
                out_ref[pl.ds(k67 * 32 + part * 2 + m, 8, stride=4), :] = sums[2 * m + part] * scale


def in_vmem():
    return pl.BlockSpec(memory_space=pltpu.VMEM)


def in_hbm():
    return pl.BlockSpec(memory_space=pltpu.HBM)


def tables(where, interpret=False):
    return pl.pallas_call(
        table_kernel,
        out_shape=[
            jax.ShapeDtypeStruct((NEAR * GC, 256, 128), BF16),
            jax.ShapeDtypeStruct((TURN + 64, 8, 128), F32),
            pltpu.HBM(((16 - NEAR) * GC, 256, 128), BF16),
            pltpu.HBM((1900, 8, 128), F32),
        ],
        in_specs=[pl.BlockSpec(memory_space=pltpu.SMEM)],
        out_specs=[in_vmem(), in_vmem(), in_hbm(), in_hbm()],
        scratch_shapes=[
            pltpu.VMEM((15, 64, 128), F32),
            pltpu.VMEM(((16 - NEAR) * GC, 256, 128), BF16),
            pltpu.VMEM((1900, 8, 128), F32),
            pltpu.VMEM((5, 8, 128), F32),
            pltpu.VMEM((5, 8, 128), F32),
            pltpu.VMEM((5, 8, 128), F32),
            pltpu.SemaphoreType.DMA((9,)),
        ],
        compiler_params=pltpu.CompilerParams(vmem_limit_bytes=14 << 20),
        interpret=interpret,
    )(where)


def contributions(where, rows, interpret=False):
    near, turn, far, table = tables(where, interpret)
    if not interpret:
        far = pltpu.with_memory_space_constraint(far, pltpu.HBM)
        table = pltpu.with_memory_space_constraint(table, pltpu.HBM)
    return pl.pallas_call(
        kernel,
        out_shape=jax.ShapeDtypeStruct((128, 128), F32),
        in_specs=[pl.BlockSpec(memory_space=pltpu.SMEM), in_vmem(), in_vmem(), in_vmem(), in_hbm(), in_hbm()],
        out_specs=in_vmem(),
        scratch_shapes=[
            pltpu.VMEM((2, 2, 16, 8, 128), F32),
            pltpu.VMEM((1280, 128), F32),
            pltpu.VMEM((2, 250, 8, 128), F32),
            pltpu.VMEM((4, 250, 8, 128), F32),
            pltpu.VMEM((100, 8, 128), F32),
            pltpu.VMEM(((16 - NEAR) * GC, 256, 128), BF16),
            pltpu.VMEM((1900, 8, 128), F32),
            pltpu.SemaphoreType.DMA((9,)),
        ],
        compiler_params=pltpu.CompilerParams(vmem_limit_bytes=20 << 20),
        interpret=interpret,
    )(where, rows, near, turn, far, table)


def shards(samples):
    rows = samples.reshape(1, 16, 128)
    rows = jnp.broadcast_to(rows, (16, 16, 128))
    rows = lax.all_to_all(rows, AXES, 0, 0, axis_index_groups=gather_groups())
    where = jnp.stack([lax.axis_index("inline"), lax.axis_index("xline")]).astype(jnp.int32)
    parts = contributions(where, rows).reshape(32, 4, 128)
    parts = lax.all_to_all(parts, AXES, 0, 0, axis_index_groups=scatter_groups())
    return jnp.sum(parts, axis=0).reshape(2, COLS)


def solution(mesh):
    return jax.shard_map(
        shards,
        mesh=mesh,
        in_specs=(P(None, "inline", "xline"),),
        out_specs=P(None, AXES),
        check_vma=False,
    )
```

time: 66.6 us -> 57.4 us (0.86)
  waiting for transfers between devices: 6.71 us -> 1.32 us
  Pallas kernels: 16.6 us -> 14.2 us
    pallas_call x1, Pallas kernels: 16.6 us -> 8.27 us  [contributions(): pl.pallas_call(kernel, out_shape=jax.ShapeDtypeStruct((128, 128), F32), i...]
    pallas_call x0 -> x1, Pallas kernels: none -> 5.92 us  [tables(): pl.pallas_call(table_kernel, out_shape=[jax.ShapeDtypeStruct((NEAR * GC,...]
    all_to_all x1, waiting for transfers between devices: 6.71 us -> 1.32 us  [shards(): rows = lax.all_to_all(rows, AXES, 0, 0, axis_index_groups=gather_groups())]
  transfers between devices with their start and end apart: 1 -> 1, of which waited for: 1 -> 1; matrix products, arithmetic and copies ran while one was open for 1% -> 0% of each run, Pallas kernels for 0% -> 10%
where the time goes in v1:
time: 57.4 us; the launch traced here: 57.1 us
  blocking collectives  29.4 us (51%)
  Pallas kernels  14.2 us (25%)
  starting transfers between devices  10.2 us (18%)
  local copies, waits for them, and re-layouts  1.95 us (3%)
  waiting for transfers between devices  1.32 us (2%)
    all_to_all x1, blocking collectives, shards(): lax.all_to_all(parts, AXES, 0, 0, axis_index_groups=scatter_groups())  29.4 us
    all_to_all x1, starting transfers between devices, shards(): rows = lax.all_to_all(rows, AXES, 0, 0, axis_index_groups=gather_groups())  10.2 us
    pallas_call x1, Pallas kernels, contributions(): pl.pallas_call(kernel, out_shape=jax.ShapeDtypeStruct((128, 128), F32), i...  8.27 us
    pallas_call x1, Pallas kernels, tables(): pl.pallas_call(table_kernel, out_shape=[jax.ShapeDtypeStruct((NEAR * GC,...  5.92 us
    broadcast_in_dim x1, local copies, waits for them, and re-layouts, shards(): rows = jnp.broadcast_to(rows, (16, 16, 128))  1.35 us
    all_to_all x1, waiting for transfers between devices, shards(): rows = lax.all_to_all(rows, AXES, 0, 0, axis_index_groups=gather_groups())  1.32 us
  transfers between devices with their start and end apart: 1, of which 1 were waited for; matrix products, arithmetic and copies ran while one was open for 0% of the time, Pallas kernels for 10%

profile of v1, /device:TPU:1, one launch (start us, length us, event | category | flops | bytes accessed | tf_op | source)
XLA Modules:
  0.0 57.1 jit_solution(13250348550691168846)
XLA Ops:
  0.0 1.4 %broadcast_in_dim.8 = f32[16,16,128]{2,1,0:T(8,128)} broadcast(f32[16,128]{1,0:T(8,128)} %bitcast.5), dimensions={1,2} | broadcast | bytes 139264 | tf_op jit(solution)/shard_map/broadcast_in_dim | solution.py:650
  1.4 10.2 %all-to-all-start = ((f32[16,16,128]{2,1,0:T(8,128)}), f32[16,16,128]{2,1,0:T(8,128)S(1)}, u32[]{:S(2)}, u32[]{:S(2)}) async-start(f32[16,16,128]{2,1,0:T(8,128)} %broadcast_in_dim.8), calls=%async_computation | async-start | bytes 262144 | tf_op jit(solution)/shard_map/all_to_all | solution.py:651
  11.5 0.1 pad_add_fusion.where_ref
  11.6 5.9 %shard_map.17 = (bf16[44,256,128]{2,1,0:T(8,128)(2,1)S(1)}, f32[104,8,128]{2,1,0:T(8,128)S(1)}, bf16[20,256,128]{2,1,0:T(8,128)(2,1)}, f32[1900,8,128]{2,1,0:T(8,128)}) custom-call(s32[2]{0:T(128)S(1)} %pad_add_fusion.where_ref), custom_call_target="tpu_custom_call" | custom-call | tf_op jit(solution)/shard_map/pallas_call | solution.py:599
  17.5 1.3 %all-to-all-done.rows_ref = f32[16,16,128]{2,1,0:T(8,128)S(1)} async-done(((f32[16,16,128]{2,1,0:T(8,128)}), f32[16,16,128]{2,1,0:T(8,128)S(1)}, u32[]{:S(2)}, u32[]{:S(2)}) %all-to-all-start) | async-done | bytes 131104 | tf_op jit(solution)/shard_map/all_to_all | solution.py:651
  18.8 8.3 %shard_map.18 = f32[128,128]{1,0:T(8,128)S(1)} custom-call(s32[2]{0:T(128)S(1)} %pad_add_fusion.where_ref, f32[16,16,128]{2,1,0:T(8,128)S(1)} %all-to-all-done.rows_ref, bf16[44,256,128]{2,1,0:T(8,128)(2,1)S(1)} %get-tuple-element.9.near_ref, f32[104,8,128]{2,1,0:T(8,128)S(1)} %get-tuple-element.10.turn_ref, ...), custom_call_target="tpu_custom_call" | custom-call | tf_op jit(solution)/shard_map/pallas_call | solution.py:628
  27.1 29.4 %all_to_all.10 = f32[32,4,128]{2,1,0:T(4,128)S(1)} all-to-all(f32[32,4,128]{2,1,0:T(4,128)S(1)} %bitcast.4), channel_id=1, replica_groups={{0,4,64,68,128,132,192,196,256,260,320,324,384,388,448,452,8,12,72,76,1..., dimensions={0} | all-to-all | bytes 131072 | tf_op jit(solution)/shard_map/all_to_all | solution.py:654
  56.5 0.6 %reshape.9 = f32[2,256]{1,0:T(2,128)} reshape(f32[4,128]{1,0:T(4,128)S(1)} %reduce_sum.9) | data formatting | bytes 4096 | tf_op jit(solution)/shard_map/reshape | solution.py:655
  (1 shorter events, 0.0 us)
Async XLA Ops:
  1.4 17.5 %all-to-all-start = ((f32[16,16,128]{2,1,0:T(8,128)}), f32[16,16,128]{2,1,0:T(8,128)S(1)}, u32[]{:S(2)}, u32[]{:S(2)}) async-start(f32[16,16,128]{2,1,0:T(8,128)} %broadcast_in_dim.8), calls=%async_computation | async-start | bytes 262144 | tf_op jit(solution)/shard_map/all_to_all | solution.py:651

commit v2 on v1

--- a/solution.py
+++ b/solution.py
@@ -1,3 +1,4 @@
+import functools
 import math
 
 import jax
@@ -73,7 +74,7 @@
     while True:
         power = 2 * n + (1 if odd else 0)
         size = (scale * bound) ** power / math.factorial(power)
-        if size < 1e-8:
+        if size < 3e-8:
             return coefs
         coefs.append((-1.0) ** n * scale**power / math.factorial(power))
         n += 1
@@ -118,9 +119,8 @@
     return (2 * bit - 1).astype(F32)
 
 
-def places(where_ref):
-    a = where_ref[0]
-    b = where_ref[1]
+def places(where):
+    a, b = where()
     lane = lax.broadcasted_iota(jnp.int32, (8, 128), 1)
     sub = lax.broadcasted_iota(jnp.int32, (8, 128), 0)
     column = lane + ((a & 1) << 7)
@@ -144,23 +144,112 @@
     return [(c3, s3), (cc - ss, sc + cs), (c2, s2), (cc + ss, sc - cs), (c1, s1)]
 
 
-SETS = ((0, 1), (1, 2), (2, 3), (3, 4), (4, 5), (5, 7), (7, 11), (11, 19))
-TURN = 40
 NEAR = 11
-
-
-def stretch(k, source, target, sem):
-    low, high = SETS[k]
-    at = pl.ds(low * 100, (high - low) * 100)
-    return pltpu.make_async_copy(source.at[at], target.at[at], sem)
-
-
-def table_kernel(where_ref, near_ref, turn_ref, far_ref, table_ref, tab_ref, far_s, table_s, p_ref, q_ref, s_ref, sems):
-    a, b, lane, sub, (g0, g1, g2) = places(where_ref)
+STRETCHES = ((7, 11), (11, 15), (15, 19))
+
+
+def stretch(k, table, held, sem, out):
+    low, high = STRETCHES[k]
+    far = table.at[pl.ds((low - 7) * 100, (high - low) * 100)]
+    near = held.at[pl.ds(low * 100, (high - low) * 100)]
+    return pltpu.make_async_copy(near, far, sem) if out else pltpu.make_async_copy(far, near, sem)
+
+
+def plan(a, b, sub, centre):
+    g0, g1, g2 = centre
+    bit2, bit1, bit0, none = sub >> 2 & 1, sub >> 1 & 1, sub & 1, sub * 0
+    a_base = a & ~3
+    b_base = b & ~3
+    unit_b = (b_base + bit2 + 2 * bit0).astype(F32) * (1.0 / N_XLINE)
+    unit_a = (a_base + 2 * bit1).astype(F32) * (1.0 / N_INLINE)
+    low_b = (b_base + 2 * bit0).astype(F32) * (1.0 / N_XLINE)
+
+    def inline_low(bits):
+        return (none + (a >> bits << bits)).astype(F32) * (1.0 / N_INLINE)
+
+    def xline_low(bits):
+        return (none + (b >> bits << bits)).astype(F32) * (1.0 / N_XLINE)
+
+    levels = []
+    sign = spot(none + (b & 1))
+    for side in range(2):
+        box = (unit_a + side / N_INLINE, 1.0 / N_INLINE, unit_b, 1.0 / N_XLINE)
+        levels.append((box, (g0, g1, g2), 2, 2.0**-4, [sign], side))
+    g2 = g2 + sign * 2.0**-4
+    sign = spot(none + (a >> 1 & 1))
+    box = (unit_a, 2.0 / N_INLINE, unit_b, 1.0 / N_XLINE)
+    levels.append((box, (g0, g1, g2), 0, 2.0**-5, [sign], 0))
+    g0 = g0 + sign * 2.0**-5
+    sign = spot(none + (b >> 1 & 1))
+    box = (unit_a, 2.0 / N_INLINE, low_b, 2.0 / N_XLINE)
+    levels.append((box, (g0, g1, g2), 1, 2.0**-5, [sign], 1))
+    g1 = g1 + sign * 2.0**-5
+    sign = spot(bit1)
+    box = (inline_low(2), 4.0 / N_INLINE, low_b, 2.0 / N_XLINE)
+    levels.append((box, (g0, g1, g2), 2, 2.0**-5, [sign], 2))
+    g2 = g2 + sign * 2.0**-5
+    sign = spot(bit0)
+    box = (inline_low(2), 4.0 / N_INLINE, xline_low(2), 4.0 / N_XLINE)
+    levels.append((box, (g0, g1, g2), 0, 2.0**-6, [sign], 3))
+    g0 = g0 + sign * 2.0**-6
+    sign = spot(bit2)
+    box = (inline_low(3), 8.0 / N_INLINE, xline_low(2), 4.0 / N_XLINE)
+    levels.append((box, (g0, g1, g2), 1, 2.0**-6, [sign], 4))
+    g1 = g1 + sign * 2.0**-6
+    box = (inline_low(3), 8.0 / N_INLINE, xline_low(3), 8.0 / N_XLINE)
+    levels.append((box, (g0, g1, g2), 2, 2.0**-6, [-1.0, 1.0], 5))
+    for k6 in range(2):
+        box = (inline_low(4), 16.0 / N_INLINE, xline_low(3), 8.0 / N_XLINE)
+        centre = (g0, g1, g2 + (2 * k6 - 1) * 2.0**-6)
+        levels.append((box, centre, 0, 2.0**-7, [-1.0, 1.0], 7 + 2 * k6))
+    for k6 in range(2):
+        for k7 in range(2):
+            box = (inline_low(4), 16.0 / N_INLINE, full(0.0), 16.0 / N_XLINE)
+            centre = (g0 + (2 * k7 - 1) * 2.0**-7, g1, g2 + (2 * k6 - 1) * 2.0**-6)
+            levels.append((box, centre, 1, 2.0**-7, [-1.0, 1.0], 11 + 4 * k6 + 2 * k7))
+    return levels
+
+
+def turning(level, slot, p_ref, q_ref, s_ref, store):
+    (low0, width0, low1, width1), centre, dim, q, signs, first = level
+    anchor = 0.5 + centre[0]
+    for k in range(5):
+        place = float(NODES[k]) + 0.5
+        x0 = (low0 + width0 * place) * (low0 + width0 * place)
+        x1 = (low1 + width1 * place) * (low1 + width1 * place)
+        p_ref[slot, k] = anchor * anchor + centre[1] * x0
+        q_ref[slot, k] = centre[2] * x1
+        if dim:
+            s_ref[slot, k] = (x0 if dim == 1 else x1) * q
+    for m, sign in enumerate(signs):
+        if dim == 0:
+            s_ref[slot, m] = 2.0 * q * sign * anchor + q * q
+
+    def point(b0, b1):
+        radicand = p_ref[slot, b0] + q_ref[slot, b1]
+        root = radicand * lax.rsqrt(radicand)
+        for m, sign in enumerate(signs):
+            if dim == 0:
+                moved = radicand + s_ref[slot, m]
+            else:
+                gap = s_ref[slot, b0 if dim == 1 else b1]
+                if isinstance(sign, float):
+                    moved = radicand + gap if sign > 0 else radicand - gap
+                else:
+                    moved = radicand + sign * gap
+            change = moved * lax.rsqrt(moved) - root
+            s_u, c_u = sincos_small(change, 0.5 * KAPPA, q)
+            s_v, c_v = sincos_small(change, KAPPA * float(NODES[1]), q)
+            store(first + m, b0, b1, (c_u, s_u, c_v, s_v))
+
+    return point
+
+
+def table_kernel(where, near_ref, turn_ref, far_ref, table_ref, tab_ref, far_s, table_s, p_ref, q_ref, s_ref, sems):
+    a, b, lane, sub, (g0, g1, g2) = places(where)
     bit2 = sub >> 2 & 1
     bit1 = sub >> 1 & 1
     bit0 = sub & 1
-    none = sub * 0
     a_base = a & ~3
     b_base = b & ~3
 
@@ -178,8 +267,8 @@
             s, co = sincos_wide(step * 132.0)
             s64, c64 = sincos_wide(step * 64.0)
             for f1 in range(4):
-                turn_ref[TURN + f1 * 16 + c * 2 + half] = co
-                turn_ref[TURN + f1 * 16 + 8 + c * 2 + half] = s
+                turn_ref[f1 * 16 + c * 2 + half] = co
+                turn_ref[f1 * 16 + 8 + c * 2 + half] = s
                 if f1 < 3:
                     co, s = cmul(co, s, c64, s64)
             s8, c8 = sincos_wide(step * 8.0)
@@ -219,151 +308,53 @@
         return carry
 
     lax.fori_loop(NEAR, 16, far_wave, 0)
-    save_far = pltpu.make_async_copy(far_s, far_ref, sems.at[8])
+    save_far = pltpu.make_async_copy(far_s, far_ref, sems.at[3])
     save_far.start()
 
-    def save(k):
-        stretch(k, table_s, table_ref, sems.at[k]).start()
-
-    def box_squares(low, width):
-        return [(low + width * (float(NODES[k]) + 0.5)) * (low + width * (float(NODES[k]) + 0.5)) for k in range(5)]
-
-    def level(low0, width0, low1, width1, centre, dim, q, sigmas, store, first=False):
-        anchor = 0.5 + centre[0]
-        x0 = box_squares(low0, width0)
-        x1 = box_squares(low1, width1)
-        for k in range(5):
-            p_ref[k] = anchor * anchor + centre[1] * x0[k]
-            q_ref[k] = centre[2] * x1[k]
-            if dim:
-                s_ref[k] = (x0 if dim == 1 else x1)[k] * q + full(0.0)
-        if dim == 0:
-            gaps = [2.0 * q * sigma * anchor + q * q for sigma in sigmas]
-
-        def body(b1, carry):
-            across = q_ref[b1]
-            for b0 in (2,) if first else range(5):
-                radicand = p_ref[b0] + across
-                root = radicand * lax.rsqrt(radicand)
-                for m, sigma in enumerate(sigmas):
-                    if dim == 0:
-                        moved = radicand + gaps[m]
-                    else:
-                        gap = s_ref[b0 if dim == 1 else b1]
-                        if isinstance(sigma, float):
-                            moved = radicand + gap if sigma > 0 else radicand - gap
-                        else:
-                            moved = radicand + sigma * gap
-                    change = moved * lax.rsqrt(moved) - root
-                    s_u, c_u = sincos_small(change, 0.5 * KAPPA, q)
-                    s_v, c_v = sincos_small(change, KAPPA * float(NODES[1]), q)
-                    store(m, b0, b1, (c_u, s_u, c_v, s_v))
+    def held(index, b0, b1, factor):
+        for k in range(4):
+            table_s[index * 100 + (b0 * 5 + b1) * 4 + k] = factor[k]
+
+    saves = []
+    for i, level in enumerate(plan(a, b, sub, (g0, g1, g2))[8:]):
+        point = turning(level, 0, p_ref, q_ref, s_ref, held)
+
+        def across(b1, carry, point=point):
+            for b0 in range(5):
+                point(b0, b1)
             return carry
 
-        lax.fori_loop(0, 5, body, 0)
-
-    def into_levels(index_of):
-        def store(m, b0, b1, factor):
-            for k in range(4):
-                table_s[index_of(m) * 100 + (b0 * 5 + b1) * 4 + k] = factor[k]
-
-        return store
-
-    unit_b = (b_base + bit2 + 2 * bit0).astype(F32) * (1.0 / N_XLINE)
-    unit_a = (a_base + 2 * bit1).astype(F32) * (1.0 / N_INLINE)
-    for side in range(2):
-
-        def into_first(m, b0, b1, factor, side=side):
-            for k in range(4):
-                turn_ref[side * 20 + b1 * 4 + k] = factor[k]
-
-        level(
-            unit_a + side / N_INLINE, 1.0 / N_INLINE, unit_b, 1.0 / N_XLINE,
-            (g0, g1, g2), 2, 2.0**-4, [spot(none + (b & 1))], into_first, True,
-        )
-    g2 = g2 + spot(none + (b & 1)) * 2.0**-4
-
-    level(
-        unit_a, 2.0 / N_INLINE, unit_b, 1.0 / N_XLINE,
-        (g0, g1, g2), 0, 2.0**-5, [spot(none + (a >> 1 & 1))], into_levels(lambda m: 0),
-    )
-    save(0)
-    g0 = g0 + spot(none + (a >> 1 & 1)) * 2.0**-5
-
-    low_b = (b_base + 2 * bit0).astype(F32) * (1.0 / N_XLINE)
-    level(
-        unit_a, 2.0 / N_INLINE, low_b, 2.0 / N_XLINE,
-        (g0, g1, g2), 1, 2.0**-5, [spot(none + (b >> 1 & 1))], into_levels(lambda m: 1),
-    )
-    save(1)
-    g1 = g1 + spot(none + (b >> 1 & 1)) * 2.0**-5
-
-    node_a = full(0.0) + a_base.astype(F32) * (1.0 / N_INLINE)
-    level(
-        node_a, 4.0 / N_INLINE, low_b, 2.0 / N_XLINE,
-        (g0, g1, g2), 2, 2.0**-5, [spot(bit1)], into_levels(lambda m: 2),
-    )
-    save(2)
-    g2 = g2 + spot(bit1) * 2.0**-5
-
-    node_b = full(0.0) + b_base.astype(F32) * (1.0 / N_XLINE)
-    level(
-        node_a, 4.0 / N_INLINE, node_b, 4.0 / N_XLINE,
-        (g0, g1, g2), 0, 2.0**-6, [spot(bit0)], into_levels(lambda m: 3),
-    )
-    save(3)
-    g0 = g0 + spot(bit0) * 2.0**-6
-
-    node_a = full(0.0) + (a & ~7).astype(F32) * (1.0 / N_INLINE)
-    level(
-        node_a, 8.0 / N_INLINE, node_b, 4.0 / N_XLINE,
-        (g0, g1, g2), 1, 2.0**-6, [spot(bit2)], into_levels(lambda m: 4),
-    )
-    save(4)
-    g1 = g1 + spot(bit2) * 2.0**-6
-
-    node_b = full(0.0) + (b & ~7).astype(F32) * (1.0 / N_XLINE)
-    level(
-        node_a, 8.0 / N_INLINE, node_b, 8.0 / N_XLINE,
-        (g0, g1, g2), 2, 2.0**-6, [-1.0, 1.0], into_levels(lambda m: 5 + m),
-    )
-    save(5)
-
-    node_a = full(0.0) + (a & ~15).astype(F32) * (1.0 / N_INLINE)
-    for k6 in range(2):
-        level(
-            node_a, 16.0 / N_INLINE, node_b, 8.0 / N_XLINE,
-            (g0, g1, g2 + (2 * k6 - 1) * 2.0**-6), 0, 2.0**-7, [-1.0, 1.0],
-            into_levels((lambda k6: lambda m: 7 + 2 * k6 + m)(k6)),
-        )
-    save(6)
-
-    for k6 in range(2):
-        for k7 in range(2):
-
-            def into_last(m, b0, b1, factor, first=11 + 4 * k6 + 2 * k7):
-                for k in range(4):
-                    table_s[(first + m) * 100 + (b0 * 5 + b1) * 4 + k] = factor[k]
-
-            level(
-                node_a, 16.0 / N_INLINE, full(0.0), 16.0 / N_XLINE,
-                (g0 + (2 * k7 - 1) * 2.0**-7, g1, g2 + (2 * k6 - 1) * 2.0**-6), 1, 2.0**-7,
-                [-1.0, 1.0], into_last,
-            )
-    save(7)
+        lax.fori_loop(0, 5, across, 0)
+        if i % 2:
+            k = i // 2
+            saves.append(stretch(k, table_ref, table_s, sems.at[k], True))
+            saves[-1].start()
     lax.fori_loop(0, NEAR, near_wave, 0)
     save_far.wait()
-    for k in range(8):
-        stretch(k, table_s, table_ref, sems.at[k]).wait()
-
-
-def kernel(where_ref, rows_ref, near_ref, turn_ref, far_ref, table_ref, out_ref, v_ref, leaf_ref, wa_ref, wb_ref, x_ref, far_s, table_s, sems):
-    load_far = pltpu.make_async_copy(far_ref, far_s, sems.at[8])
+    for copy in saves:
+        copy.wait()
+
+
+def kernel(where, rows_ref, near_ref, turn_ref, far_ref, table_ref, out_ref, v_ref, leaf_ref, wa_ref, wb_ref, x_ref, far_s, table_s, first_s, p_ref, q_ref, s_ref, sems):
+    load_far = pltpu.make_async_copy(far_ref, far_s, sems.at[3])
     load_far.start()
-    loads = [stretch(k, table_ref, table_s, sems.at[k]) for k in range(8)]
+    loads = [stretch(k, table_ref, table_s, sems.at[k], False) for k in range(3)]
     for load in loads:
         load.start()
-    a, b, lane, sub, unused = places(where_ref)
+    a, b, lane, sub, kept = places(where)
+
+    def hold_first(side, b0, b1, factor):
+        for k in range(4):
+            first_s[side * 20 + b1 * 4 + k] = factor[k]
+
+    def hold(index, b0, b1, factor):
+        for k in range(4):
+            table_s[index * 100 + (b0 * 5 + b1) * 4 + k] = factor[k]
+
+    points = []
+    for i, level in enumerate(plan(a, b, sub, kept)[:8]):
+        point = turning(level, i, p_ref, q_ref, s_ref, hold_first if i < 2 else hold)
+        points += [(point, b0, b1) for b0 in ((2,) if i < 2 else range(5)) for b1 in range(5)]
 
     left = lax.broadcasted_iota(jnp.int32, (16, 8, 128), 2) < 64
     re = rows_ref[:, 0:8, :]
@@ -393,7 +384,7 @@
         totals = []
         for c in range(GC):
             def table(i):
-                return jnp.broadcast_to(turn_ref[TURN + i * 8 + c * 2 + box // 8, pl.ds(box % 8, 1), :], (8, 128))
+                return jnp.broadcast_to(turn_ref[i * 8 + c * 2 + box // 8, pl.ds(box % 8, 1), :], (8, 128))
 
             rows = []
             for f1 in range(4):
@@ -425,6 +416,8 @@
         if box == NEAR:
             load_far.wait()
         leaf_one(box)
+        for point, b0, b1 in points[box::16]:
+            point(b0, b1)
 
     def merge(axis, points, sets, read, turn, weight, write, combine):
         def body(other, carry):
@@ -511,46 +504,40 @@
 
     merge(
         0, [(0, 2), (1, 2)], 1, leaf_read,
-        lambda m, side, b0, b1: [turn_ref[side * 20 + b1 * 4 + k] for k in range(4)],
+        lambda m, side, b0, b1: [first_s[side * 20 + b1 * 4 + k] for k in range(4)],
         lambda i, side, j: float(CHILD[side][i, j]),
         writer(wa_ref, lambda m: 0), lambda v: v,
     )
-    loads[0].wait()
     merge(
         1, line, 1, reader(wa_ref, 0), turner(lambda m: 0), chosen((sub >> 2 & 1) == 1),
         writer(wb_ref, lambda m: 0), lambda v: v + pltpu.roll(v, 4, 0),
     )
-    loads[1].wait()
     merge(
         0, line, 1, reader(wb_ref, 0), turner(lambda m: 1), chosen((sub >> 1 & 1) == 1),
         writer(wa_ref, lambda m: 0), lambda v: v + pltpu.roll(v, 2, 0),
     )
-    loads[2].wait()
     even = (sub & 1) == 0
     merge(
         1, line, 1, reader(wa_ref, 0), turner(lambda m: 2), chosen((sub & 1) == 1),
         writer(wb_ref, lambda m: 0),
         lambda v: v + jnp.where(even, pltpu.roll(v, 7, 0), pltpu.roll(v, 1, 0)),
     )
-    loads[3].wait()
     order = flipped(0, a >> 2 & 1)
     merge(
         0, line, 1, reader(wb_ref, 0, order), turner(lambda m: 3, order), lower,
         writer(wa_ref, lambda m: 0, order), lambda v: v,
     )
-    loads[4].wait()
     order = flipped(1, b >> 2 & 1)
     merge(
         1, line, 1, reader(wa_ref, 0, order), turner(lambda m: 4, order), lower,
         writer(wb_ref, lambda m: 0, order), lambda v: v,
     )
-    loads[5].wait()
     order = flipped(0, a >> 3 & 1)
     merge(
         0, line, 2, reader(wb_ref, 0, order), turner(lambda m: 5 + m, order), lower,
         writer(wa_ref, lambda m: m, order), lambda v: v,
     )
-    loads[6].wait()
+    loads[0].wait()
     order = flipped(1, b >> 3 & 1)
     for k6 in range(2):
         merge(
@@ -559,7 +546,8 @@
             writer(wb_ref, (lambda k6: lambda m: 2 * k6 + m)(k6), order), lambda v: v,
         )
 
-    loads[7].wait()
+    loads[1].wait()
+    loads[2].wait()
     scale = 1.0 / math.sqrt(GC * NF * N_INLINE * N_XLINE)
     for k67 in range(4):
         read = reader(wb_ref, k67)
@@ -595,40 +583,62 @@
     return pl.BlockSpec(memory_space=pltpu.HBM)
 
 
-def tables(where, interpret=False):
+def device_place():
+    return lax.axis_index("inline"), lax.axis_index("xline")
+
+
+def told(body):
+    def with_place(where_ref, *refs):
+        body(lambda: (where_ref[0], where_ref[1]), *refs)
+
+    return with_place
+
+
+def run(body, where, in_specs, operands, **settings):
+    if where is None:
+        return pl.pallas_call(functools.partial(body, device_place), in_specs=in_specs, **settings)(*operands)
     return pl.pallas_call(
+        told(body), in_specs=[pl.BlockSpec(memory_space=pltpu.SMEM)] + in_specs, interpret=True, **settings
+    )(where, *operands)
+
+
+def tables(where):
+    return run(
         table_kernel,
+        where,
+        [],
+        [],
         out_shape=[
             jax.ShapeDtypeStruct((NEAR * GC, 256, 128), BF16),
-            jax.ShapeDtypeStruct((TURN + 64, 8, 128), F32),
+            jax.ShapeDtypeStruct((64, 8, 128), F32),
             pltpu.HBM(((16 - NEAR) * GC, 256, 128), BF16),
-            pltpu.HBM((1900, 8, 128), F32),
+            pltpu.HBM((1200, 8, 128), F32),
         ],
-        in_specs=[pl.BlockSpec(memory_space=pltpu.SMEM)],
         out_specs=[in_vmem(), in_vmem(), in_hbm(), in_hbm()],
         scratch_shapes=[
             pltpu.VMEM((15, 64, 128), F32),
             pltpu.VMEM(((16 - NEAR) * GC, 256, 128), BF16),
             pltpu.VMEM((1900, 8, 128), F32),
-            pltpu.VMEM((5, 8, 128), F32),
-            pltpu.VMEM((5, 8, 128), F32),
-            pltpu.VMEM((5, 8, 128), F32),
-            pltpu.SemaphoreType.DMA((9,)),
+            pltpu.VMEM((1, 5, 8, 128), F32),
+            pltpu.VMEM((1, 5, 8, 128), F32),
+            pltpu.VMEM((1, 5, 8, 128), F32),
+            pltpu.SemaphoreType.DMA((4,)),
         ],
         compiler_params=pltpu.CompilerParams(vmem_limit_bytes=14 << 20),
-        interpret=interpret,
-    )(where)
-
-
-def contributions(where, rows, interpret=False):
-    near, turn, far, table = tables(where, interpret)
-    if not interpret:
+    )
+
+
+def contributions(where, rows):
+    near, turn, far, table = tables(where)
+    if where is None:
         far = pltpu.with_memory_space_constraint(far, pltpu.HBM)
         table = pltpu.with_memory_space_constraint(table, pltpu.HBM)
-    return pl.pallas_call(
+    return run(
         kernel,
+        where,
+        [in_vmem(), in_vmem(), in_vmem(), in_hbm(), in_hbm()],
+        [rows, near, turn, far, table],
         out_shape=jax.ShapeDtypeStruct((128, 128), F32),
-        in_specs=[pl.BlockSpec(memory_space=pltpu.SMEM), in_vmem(), in_vmem(), in_vmem(), in_hbm(), in_hbm()],
         out_specs=in_vmem(),
         scratch_shapes=[
             pltpu.VMEM((2, 2, 16, 8, 128), F32),
@@ -638,19 +648,21 @@
             pltpu.VMEM((100, 8, 128), F32),
             pltpu.VMEM(((16 - NEAR) * GC, 256, 128), BF16),
             pltpu.VMEM((1900, 8, 128), F32),
-            pltpu.SemaphoreType.DMA((9,)),
+            pltpu.VMEM((40, 8, 128), F32),
+            pltpu.VMEM((8, 5, 8, 128), F32),
+            pltpu.VMEM((8, 5, 8, 128), F32),
+            pltpu.VMEM((8, 5, 8, 128), F32),
+            pltpu.SemaphoreType.DMA((4,)),
         ],
         compiler_params=pltpu.CompilerParams(vmem_limit_bytes=20 << 20),
-        interpret=interpret,
-    )(where, rows, near, turn, far, table)
+    )
 
 
 def shards(samples):
     rows = samples.reshape(1, 16, 128)
     rows = jnp.broadcast_to(rows, (16, 16, 128))
     rows = lax.all_to_all(rows, AXES, 0, 0, axis_index_groups=gather_groups())
-    where = jnp.stack([lax.axis_index("inline"), lax.axis_index("xline")]).astype(jnp.int32)
-    parts = contributions(where, rows).reshape(32, 4, 128)
+    parts = contributions(None, rows).reshape(32, 4, 128)
     parts = lax.all_to_all(parts, AXES, 0, 0, axis_index_groups=scatter_groups())
     return jnp.sum(parts, axis=0).reshape(2, COLS)
 

time: 57.4 us -> 57.5 us (level)
  waiting for transfers between devices: 1.32 us -> 4.01 us
  Pallas kernels: 14.2 us -> 11.7 us
    all_to_all x1, waiting for transfers between devices: 1.32 us -> 4.01 us  [shards(): rows = lax.all_to_all(rows, AXES, 0, 0, axis_index_groups=gather_groups())]
    pallas_call x2, Pallas kernels: 14.2 us -> 11.7 us  [run(): pl.pallas_call(functools.partial(body, device_place), in_specs=in_specs,...]
  transfers between devices with their start and end apart: 1 -> 1, of which waited for: 1 -> 1; matrix products, arithmetic and copies ran while one was open for 0% -> 0% of each run, Pallas kernels for 10% -> 6%
where the time goes in v2:
time: 57.5 us; the launch traced here: 57.3 us
  blocking collectives  29.4 us (51%)
  Pallas kernels  11.7 us (20%)
  starting transfers between devices  10.2 us (18%)
  waiting for transfers between devices  4.01 us (7%)
  local copies, waits for them, and re-layouts  1.96 us (3%)
    all_to_all x1, blocking collectives, shards(): lax.all_to_all(parts, AXES, 0, 0, axis_index_groups=scatter_groups())  29.4 us
    pallas_call x2, Pallas kernels, run(): pl.pallas_call(functools.partial(body, device_place), in_specs=in_specs,...  11.7 us
    all_to_all x1, starting transfers between devices, shards(): rows = lax.all_to_all(rows, AXES, 0, 0, axis_index_groups=gather_groups())  10.2 us
    all_to_all x1, waiting for transfers between devices, shards(): rows = lax.all_to_all(rows, AXES, 0, 0, axis_index_groups=gather_groups())  4.01 us
    broadcast_in_dim x1, local copies, waits for them, and re-layouts, shards(): rows = jnp.broadcast_to(rows, (16, 16, 128))  1.36 us
  transfers between devices with their start and end apart: 1, of which 1 were waited for; matrix products, arithmetic and copies ran while one was open for 0% of the time, Pallas kernels for 6%

profile of v2, /device:TPU:1, one launch (start us, length us, event | category | flops | bytes accessed | tf_op | source)
XLA Modules:
  0.0 57.3 jit_solution(3587158686193804316)
XLA Ops:
  0.0 1.4 %broadcast_in_dim.8 = f32[16,16,128]{2,1,0:T(8,128)} broadcast(f32[16,128]{1,0:T(8,128)} %bitcast.3), dimensions={1,2} | broadcast | bytes 139264 | tf_op jit(solution)/shard_map/broadcast_in_dim | solution.py:663
  1.4 10.2 %all-to-all-start = ((f32[16,16,128]{2,1,0:T(8,128)}), f32[16,16,128]{2,1,0:T(8,128)S(1)}, u32[]{:S(2)}, u32[]{:S(2)}) async-start(f32[16,16,128]{2,1,0:T(8,128)} %broadcast_in_dim.8), calls=%async_computation | async-start | bytes 262144 | tf_op jit(solution)/shard_map/all_to_all | solution.py:664
  11.5 3.3 %shard_map.17 = (bf16[44,256,128]{2,1,0:T(8,128)(2,1)S(1)}, f32[64,8,128]{2,1,0:T(8,128)S(1)}, bf16[20,256,128]{2,1,0:T(8,128)(2,1)}, f32[1200,8,128]{2,1,0:T(8,128)}) custom-call(), custom_call_target="tpu_custom_call" | custom-call | tf_op jit(solution)/shard_map/pallas_call | solution.py:599
  14.8 4.0 %all-to-all-done.rows_ref = f32[16,16,128]{2,1,0:T(8,128)S(1)} async-done(((f32[16,16,128]{2,1,0:T(8,128)}), f32[16,16,128]{2,1,0:T(8,128)S(1)}, u32[]{:S(2)}, u32[]{:S(2)}) %all-to-all-start) | async-done | bytes 131104 | tf_op jit(solution)/shard_map/all_to_all | solution.py:664
  18.8 8.4 %shard_map.18 = f32[128,128]{1,0:T(8,128)S(1)} custom-call(f32[16,16,128]{2,1,0:T(8,128)S(1)} %all-to-all-done.rows_ref, bf16[44,256,128]{2,1,0:T(8,128)(2,1)S(1)} %get-tuple-element.9.near_ref, f32[64,8,128]{2,1,0:T(8,128)S(1)} %get-tuple-element.10.turn_ref, bf16[20,256,128]{2,1,0:T(8,128)(2,1)} %get-tuple-element.11.far_ref, ...), custom_call_target="tpu_custom_call" | custom-call | tf_op jit(solution)/shard_map/pallas_call | solution.py:599
  27.3 29.4 %all_to_all.10 = f32[32,4,128]{2,1,0:T(4,128)S(1)} all-to-all(f32[32,4,128]{2,1,0:T(4,128)S(1)} %bitcast.2), channel_id=1, replica_groups={{0,4,64,68,128,132,192,196,256,260,320,324,384,388,448,452,8,12,72,76,1..., dimensions={0} | all-to-all | bytes 131072 | tf_op jit(solution)/shard_map/all_to_all | solution.py:666
  56.7 0.6 %reshape.9 = f32[2,256]{1,0:T(2,128)} reshape(f32[4,128]{1,0:T(4,128)S(1)} %reduce_sum.9) | data formatting | bytes 4096 | tf_op jit(solution)/shard_map/reshape | solution.py:667
  (1 shorter events, 0.0 us)
Async XLA Ops:
  1.4 17.5 %all-to-all-start = ((f32[16,16,128]{2,1,0:T(8,128)}), f32[16,16,128]{2,1,0:T(8,128)S(1)}, u32[]{:S(2)}, u32[]{:S(2)}) async-start(f32[16,16,128]{2,1,0:T(8,128)} %broadcast_in_dim.8), calls=%async_computation | async-start | bytes 262144 | tf_op jit(solution)/shard_map/all_to_all | solution.py:664

commit v3 on v2

--- a/solution.py
+++ b/solution.py
@@ -210,7 +210,7 @@
     return levels
 
 
-def turning(level, slot, p_ref, q_ref, s_ref, store):
+def turning(level, slot, p_ref, q_ref, s_ref, store, part=None):
     (low0, width0, low1, width1), centre, dim, q, signs, first = level
     anchor = 0.5 + centre[0]
     for k in range(5):
@@ -238,6 +238,8 @@
                 else:
                     moved = radicand + sign * gap
             change = moved * lax.rsqrt(moved) - root
+            if part is not None:
+                change = change * part
             s_u, c_u = sincos_small(change, 0.5 * KAPPA, q)
             s_v, c_v = sincos_small(change, KAPPA * float(NODES[1]), q)
             store(first + m, b0, b1, (c_u, s_u, c_v, s_v))
@@ -307,7 +309,7 @@
         wave(box, near_ref, 0)
         return carry
 
-    lax.fori_loop(NEAR, 16, far_wave, 0)
+    lax.fori_loop(NEAR, 16, far_wave, 0, unroll=True)
     save_far = pltpu.make_async_copy(far_s, far_ref, sems.at[3])
     save_far.start()
 
@@ -324,12 +326,12 @@
                 point(b0, b1)
             return carry
 
-        lax.fori_loop(0, 5, across, 0)
+        lax.fori_loop(0, 5, across, 0, unroll=True)
         if i % 2:
             k = i // 2
             saves.append(stretch(k, table_ref, table_s, sems.at[k], True))
             saves[-1].start()
-    lax.fori_loop(0, NEAR, near_wave, 0)
+    lax.fori_loop(0, NEAR, near_wave, 0, unroll=True)
     save_far.wait()
     for copy in saves:
         copy.wait()
@@ -351,9 +353,14 @@
         for k in range(4):
             table_s[index * 100 + (b0 * 5 + b1) * 4 + k] = factor[k]
 
+    upper = (sub >> 2 & 1) == 1
+    part = jnp.where(upper, 1.0, -1.0)
+
     points = []
     for i, level in enumerate(plan(a, b, sub, kept)[:8]):
-        point = turning(level, i, p_ref, q_ref, s_ref, hold_first if i < 2 else hold)
+        point = turning(
+            level, i, p_ref, q_ref, s_ref, hold_first if i < 2 else hold, part if i in (3, 4, 5) else None
+        )
         points += [(point, b0, b1) for b0 in ((2,) if i < 2 else range(5)) for b1 in range(5)]
 
     left = lax.broadcasted_iota(jnp.int32, (16, 8, 128), 2) < 64
@@ -419,7 +426,7 @@
         for point, b0, b1 in points[box::16]:
             point(b0, b1)
 
-    def merge(axis, points, sets, read, turn, weight, write, combine):
+    def merge(axis, points, sets, read, turn, weight, write):
         def body(other, carry):
             for n, (side, p) in enumerate(points):
                 b0, b1 = (p, other) if axis == 0 else (other, p)
@@ -431,21 +438,72 @@
                         x_ref[(m * 5 + n) * 10 + 2 * b2] = x_re
                         x_ref[(m * 5 + n) * 10 + 2 * b2 + 1] = x_im
             for m in range(sets):
-                for comp in range(10):
-                    items = [x_ref[(m * 5 + n) * 10 + comp] for n in range(len(points))]
+                for b2 in range(5):
+                    items = [
+                        [x_ref[(m * 5 + n) * 10 + 2 * b2 + k] for n in range(len(points))] for k in range(2)
+                    ]
                     for i in range(5):
-                        total = None
-                        for (side, p), item in zip(points, items):
-                            coef = weight(i, side, p)
-                            if coef is None:
-                                continue
-                            term = item if isinstance(coef, float) and coef == 1.0 else item * coef
-                            total = term if total is None else total + term
+                        totals = []
+                        for k in range(2):
+                            total = None
+                            for (side, p), item in zip(points, items[k]):
+                                coef = weight(i, side, p)
+                                if coef is None:
+                                    continue
+                                term = item if isinstance(coef, float) and coef == 1.0 else item * coef
+                                total = term if total is None else total + term
+                            totals.append(total)
                         i0, i1 = (i, other) if axis == 0 else (other, i)
-                        write(m, i0, i1, comp, combine(total))
+                        write(m, i0, i1, b2, totals)
             return carry
 
         lax.fori_loop(0, 5, body, 0)
+
+    def merge_packed(axis, weight, read, turn, write, combine):
+        def body(other, carry):
+            for b in range(5):
+                b0, b1 = (b, other) if axis == 0 else (other, b)
+                for b2, (co, sine) in enumerate(five(turn(0, 0, b0, b1))):
+                    both = read(b0, b1, b2)
+                    x_ref[b * 5 + b2] = both * co + pltpu.roll(both, 4, 0) * sine
+            for b2 in range(5):
+                items = [x_ref[b * 5 + b2] for b in range(5)]
+                for i in range(5):
+                    total = None
+                    for b in range(5):
+                        coef = weight(i, 0, b)
+                        if coef is None:
+                            continue
+                        term = items[b] if isinstance(coef, float) and coef == 1.0 else items[b] * coef
+                        total = term if total is None else total + term
+                    i0, i1 = (i, other) if axis == 0 else (other, i)
+                    write(i0, i1, b2, combine(total))
+            return carry
+
+        lax.fori_loop(0, 5, body, 0)
+
+    def packed_reader(ref, order=None):
+        def read(b0, b1, b2):
+            b0, b1 = (b0, b1) if order is None else order(b0, b1)
+            return ref[0, (b0 * 5 + b1) * 10 + b2]
+
+        return read
+
+    def packed_writer(ref, order=None):
+        def write(i0, i1, b2, value):
+            i0, i1 = (i0, i1) if order is None else order(i0, i1)
+            ref[0, (i0 * 5 + i1) * 10 + b2] = value
+
+        return write
+
+    def unpacked_reader(ref, order):
+        def read(side, b0, b1, b2):
+            b0, b1 = order(b0, b1)
+            both = ref[0, (b0 * 5 + b1) * 10 + b2]
+            turned = pltpu.roll(both, 4, 0)
+            return jnp.where(upper, turned, both), jnp.where(upper, both, turned)
+
+        return read
 
     def chosen(mask):
         table = [
@@ -490,9 +548,10 @@
         return turn
 
     def writer(ref, index_of, order=same):
-        def write(m, i0, i1, comp, value):
+        def write(m, i0, i1, b2, totals):
             i0, i1 = order(i0, i1)
-            ref[index_of(m), (i0 * 5 + i1) * 10 + comp] = value
+            for k in range(2):
+                ref[index_of(m), (i0 * 5 + i1) * 10 + 2 * b2 + k] = totals[k]
 
         return write
 
@@ -506,36 +565,38 @@
         0, [(0, 2), (1, 2)], 1, leaf_read,
         lambda m, side, b0, b1: [first_s[side * 20 + b1 * 4 + k] for k in range(4)],
         lambda i, side, j: float(CHILD[side][i, j]),
-        writer(wa_ref, lambda m: 0), lambda v: v,
-    )
-    merge(
-        1, line, 1, reader(wa_ref, 0), turner(lambda m: 0), chosen((sub >> 2 & 1) == 1),
-        writer(wb_ref, lambda m: 0), lambda v: v + pltpu.roll(v, 4, 0),
-    )
-    merge(
-        0, line, 1, reader(wb_ref, 0), turner(lambda m: 1), chosen((sub >> 1 & 1) == 1),
-        writer(wa_ref, lambda m: 0), lambda v: v + pltpu.roll(v, 2, 0),
+        writer(wa_ref, lambda m: 0),
+    )
+    def pack(m, i0, i1, b2, totals):
+        re, im = totals
+        both = jnp.where(upper, im, re) + pltpu.roll(jnp.where(upper, re, im), 4, 0)
+        wb_ref[0, (i0 * 5 + i1) * 10 + b2] = both
+
+    merge(1, line, 1, reader(wa_ref, 0), turner(lambda m: 0), chosen(upper), pack)
+    odd = (sub >> 1 & 1) == 1
+    merge_packed(
+        0, chosen(odd), packed_reader(wb_ref), turner(lambda m: 1), packed_writer(wa_ref),
+        lambda v: v + jnp.where(odd, pltpu.roll(v, 2, 0), pltpu.roll(v, 6, 0)),
     )
     even = (sub & 1) == 0
-    merge(
-        1, line, 1, reader(wa_ref, 0), turner(lambda m: 2), chosen((sub & 1) == 1),
-        writer(wb_ref, lambda m: 0),
+    merge_packed(
+        1, chosen((sub & 1) == 1), packed_reader(wa_ref), turner(lambda m: 2), packed_writer(wb_ref),
         lambda v: v + jnp.where(even, pltpu.roll(v, 7, 0), pltpu.roll(v, 1, 0)),
     )
     order = flipped(0, a >> 2 & 1)
-    merge(
-        0, line, 1, reader(wb_ref, 0, order), turner(lambda m: 3, order), lower,
-        writer(wa_ref, lambda m: 0, order), lambda v: v,
+    merge_packed(
+        0, lower, packed_reader(wb_ref, order), turner(lambda m: 3, order), packed_writer(wa_ref, order),
+        lambda v: v,
     )
     order = flipped(1, b >> 2 & 1)
     merge(
-        1, line, 1, reader(wa_ref, 0, order), turner(lambda m: 4, order), lower,
-        writer(wb_ref, lambda m: 0, order), lambda v: v,
+        1, line, 1, unpacked_reader(wa_ref, order), turner(lambda m: 4, order), lower,
+        writer(wb_ref, lambda m: 0, order),
     )
     order = flipped(0, a >> 3 & 1)
     merge(
         0, line, 2, reader(wb_ref, 0, order), turner(lambda m: 5 + m, order), lower,
-        writer(wa_ref, lambda m: m, order), lambda v: v,
+        writer(wa_ref, lambda m: m, order),
     )
     loads[0].wait()
     order = flipped(1, b >> 3 & 1)
@@ -543,7 +604,7 @@
         merge(
             1, line, 2, reader(wa_ref, k6, order),
             turner((lambda k6: lambda m: 7 + 2 * k6 + m)(k6), order), lower,
-            writer(wb_ref, (lambda k6: lambda m: 2 * k6 + m)(k6), order), lambda v: v,
+            writer(wb_ref, (lambda k6: lambda m: 2 * k6 + m)(k6), order),
         )
 
     loads[1].wait()

time: 57.5 us -> 57.1 us (level)
  Pallas kernels: 11.7 us -> 11.1 us
where the time goes in v3:
time: 57.1 us; the launch traced here: 56.8 us
  blocking collectives  29.4 us (51%)
  Pallas kernels  11.1 us (19%)
  starting transfers between devices  10.2 us (18%)
  waiting for transfers between devices  4.15 us (7%)
  local copies, waits for them, and re-layouts  1.96 us (3%)
    all_to_all x1, blocking collectives, shards(): lax.all_to_all(parts, AXES, 0, 0, axis_index_groups=scatter_groups())  29.4 us
    pallas_call x2, Pallas kernels, run(): pl.pallas_call(functools.partial(body, device_place), in_specs=in_specs,...  11.1 us
    all_to_all x1, starting transfers between devices, shards(): rows = lax.all_to_all(rows, AXES, 0, 0, axis_index_groups=gather_groups())  10.2 us
    all_to_all x1, waiting for transfers between devices, shards(): rows = lax.all_to_all(rows, AXES, 0, 0, axis_index_groups=gather_groups())  4.15 us
    broadcast_in_dim x1, local copies, waits for them, and re-layouts, shards(): rows = jnp.broadcast_to(rows, (16, 16, 128))  1.36 us
  transfers between devices with their start and end apart: 1, of which 1 were waited for; matrix products, arithmetic and copies ran while one was open for 0% of the time, Pallas kernels for 6%

profile of v3, /device:TPU:1, one launch (start us, length us, event | category | flops | bytes accessed | tf_op | source)
XLA Modules:
  0.0 56.8 jit_solution(9941222866017908653)
XLA Ops:
  0.0 1.4 %broadcast_in_dim.8 = f32[16,16,128]{2,1,0:T(8,128)} broadcast(f32[16,128]{1,0:T(8,128)} %bitcast.3), dimensions={1,2} | broadcast | bytes 139264 | tf_op jit(solution)/shard_map/broadcast_in_dim | solution.py:724
  1.4 10.2 %all-to-all-start = ((f32[16,16,128]{2,1,0:T(8,128)}), f32[16,16,128]{2,1,0:T(8,128)S(1)}, u32[]{:S(2)}, u32[]{:S(2)}) async-start(f32[16,16,128]{2,1,0:T(8,128)} %broadcast_in_dim.8), calls=%async_computation | async-start | bytes 262144 | tf_op jit(solution)/shard_map/all_to_all | solution.py:725
  11.5 3.2 %shard_map.17 = (bf16[44,256,128]{2,1,0:T(8,128)(2,1)S(1)}, f32[64,8,128]{2,1,0:T(8,128)S(1)}, bf16[20,256,128]{2,1,0:T(8,128)(2,1)}, f32[1200,8,128]{2,1,0:T(8,128)}) custom-call(), custom_call_target="tpu_custom_call" | custom-call | tf_op jit(solution)/shard_map/pallas_call | solution.py:660
  14.7 4.2 %all-to-all-done.rows_ref = f32[16,16,128]{2,1,0:T(8,128)S(1)} async-done(((f32[16,16,128]{2,1,0:T(8,128)}), f32[16,16,128]{2,1,0:T(8,128)S(1)}, u32[]{:S(2)}, u32[]{:S(2)}) %all-to-all-start) | async-done | bytes 131104 | tf_op jit(solution)/shard_map/all_to_all | solution.py:725
  18.8 8.0 %shard_map.18 = f32[128,128]{1,0:T(8,128)S(1)} custom-call(f32[16,16,128]{2,1,0:T(8,128)S(1)} %all-to-all-done.rows_ref, bf16[44,256,128]{2,1,0:T(8,128)(2,1)S(1)} %get-tuple-element.9.near_ref, f32[64,8,128]{2,1,0:T(8,128)S(1)} %get-tuple-element.10.turn_ref, bf16[20,256,128]{2,1,0:T(8,128)(2,1)} %get-tuple-element.11.far_ref, ...), custom_call_target="tpu_custom_call" | custom-call | tf_op jit(solution)/shard_map/pallas_call | solution.py:660
  26.8 29.4 %all_to_all.10 = f32[32,4,128]{2,1,0:T(4,128)S(1)} all-to-all(f32[32,4,128]{2,1,0:T(4,128)S(1)} %bitcast.2), channel_id=1, replica_groups={{0,4,64,68,128,132,192,196,256,260,320,324,384,388,448,452,8,12,72,76,1..., dimensions={0} | all-to-all | bytes 131072 | tf_op jit(solution)/shard_map/all_to_all | solution.py:727
  56.3 0.6 %reshape.9 = f32[2,256]{1,0:T(2,128)} reshape(f32[4,128]{1,0:T(4,128)S(1)} %reduce_sum.9) | data formatting | bytes 4096 | tf_op jit(solution)/shard_map/reshape | solution.py:728
  (1 shorter events, 0.0 us)
Async XLA Ops:
  1.4 17.5 %all-to-all-start = ((f32[16,16,128]{2,1,0:T(8,128)}), f32[16,16,128]{2,1,0:T(8,128)S(1)}, u32[]{:S(2)}, u32[]{:S(2)}) async-start(f32[16,16,128]{2,1,0:T(8,128)} %broadcast_in_dim.8), calls=%async_computation | async-start | bytes 262144 | tf_op jit(solution)/shard_map/all_to_all | solution.py:725

commit v4 on v3

--- a/solution.py
+++ b/solution.py
@@ -38,6 +38,14 @@
 LEAF_XLINE = basis_at((np.arange(GC) + 0.5) / GC - 0.5)
 
 
+FIRST_LEAD = 15
+LEAD = 25
+
+
+def wanted(index, place):
+    return (index ^ LEAD) >> place & 1
+
+
 def gather_groups():
     groups = []
     for base in range(N_INLINE * N_XLINE):
@@ -46,7 +54,7 @@
             continue
         members = []
         for j in range(16):
-            a0, b0, a1, b1 = j >> 3 & 1, j >> 2 & 1, j >> 1 & 1, j & 1
+            a0, b0, a1, b1 = (((j ^ FIRST_LEAD) >> place) & 1 for place in (3, 2, 1, 0))
             members.append((a | a0 | a1 << 1) * N_XLINE + (b | b0 | b1 << 1))
         groups.append(members)
     return groups
@@ -60,7 +68,7 @@
             continue
         members = []
         for j in range(32):
-            k6, k7, k5, k3, k4 = j >> 4 & 1, j >> 3 & 1, j >> 2 & 1, j >> 1 & 1, j & 1
+            k6, k7, k5, k3, k4 = (wanted(j, place) for place in (4, 3, 2, 1, 0))
             members.append(
                 (a | k3 << 2 | k5 << 3 | k7 << 4) * N_XLINE + (b | k4 << 2 | k6 << 3)
             )
@@ -184,28 +192,30 @@
     box = (unit_a, 2.0 / N_INLINE, low_b, 2.0 / N_XLINE)
     levels.append((box, (g0, g1, g2), 1, 2.0**-5, [sign], 1))
     g1 = g1 + sign * 2.0**-5
-    sign = spot(bit1)
+    sign = spot(bit1 ^ wanted(0, 1))
     box = (inline_low(2), 4.0 / N_INLINE, low_b, 2.0 / N_XLINE)
     levels.append((box, (g0, g1, g2), 2, 2.0**-5, [sign], 2))
     g2 = g2 + sign * 2.0**-5
-    sign = spot(bit0)
+    sign = spot(bit0 ^ wanted(0, 0))
     box = (inline_low(2), 4.0 / N_INLINE, xline_low(2), 4.0 / N_XLINE)
     levels.append((box, (g0, g1, g2), 0, 2.0**-6, [sign], 3))
     g0 = g0 + sign * 2.0**-6
-    sign = spot(bit2)
+    sign = spot(bit2 ^ wanted(0, 2))
     box = (inline_low(3), 8.0 / N_INLINE, xline_low(2), 4.0 / N_XLINE)
     levels.append((box, (g0, g1, g2), 1, 2.0**-6, [sign], 4))
     g1 = g1 + sign * 2.0**-6
     box = (inline_low(3), 8.0 / N_INLINE, xline_low(3), 8.0 / N_XLINE)
-    levels.append((box, (g0, g1, g2), 2, 2.0**-6, [-1.0, 1.0], 5))
+    signs = [2.0 * wanted(k << 4, 4) - 1.0 for k in range(2)]
+    levels.append((box, (g0, g1, g2), 2, 2.0**-6, signs, 5))
+    next_signs = [2.0 * wanted(k << 3, 3) - 1.0 for k in range(2)]
     for k6 in range(2):
         box = (inline_low(4), 16.0 / N_INLINE, xline_low(3), 8.0 / N_XLINE)
-        centre = (g0, g1, g2 + (2 * k6 - 1) * 2.0**-6)
-        levels.append((box, centre, 0, 2.0**-7, [-1.0, 1.0], 7 + 2 * k6))
+        centre = (g0, g1, g2 + signs[k6] * 2.0**-6)
+        levels.append((box, centre, 0, 2.0**-7, next_signs, 7 + 2 * k6))
     for k6 in range(2):
         for k7 in range(2):
             box = (inline_low(4), 16.0 / N_INLINE, full(0.0), 16.0 / N_XLINE)
-            centre = (g0 + (2 * k7 - 1) * 2.0**-7, g1, g2 + (2 * k6 - 1) * 2.0**-6)
+            centre = (g0 + next_signs[k7] * 2.0**-7, g1, g2 + signs[k6] * 2.0**-6)
             levels.append((box, centre, 1, 2.0**-7, [-1.0, 1.0], 11 + 4 * k6 + 2 * k7))
     return levels
 
@@ -396,7 +406,7 @@
             rows = []
             for f1 in range(4):
                 for part in range(2):
-                    sample = v_ref[f1 & 1, part, pl.ds(box, 1), 2 * c + f1 // 2, :]
+                    sample = v_ref[f1 & 1, part, pl.ds(box ^ FIRST_LEAD, 1), 2 * c + f1 // 2, :]
                     rows.append(basis[f1] * jnp.broadcast_to(sample, (8, 128)))
             lhs = jnp.concatenate(rows, axis=0)
             lhs_hi = lhs.astype(BF16)

time: 57.1 us -> 46.6 us (0.82)
  blocking collectives: 29.4 us -> 19.9 us
  waiting for transfers between devices: 4.15 us -> 0.01 us
  starting transfers between devices: 10.2 us -> 12.8 us
    all_to_all x1, blocking collectives: 29.4 us -> 19.9 us  [shards(): lax.all_to_all(parts, AXES, 0, 0, axis_index_groups=scatter_groups())]
    all_to_all x1, waiting for transfers between devices: 4.15 us -> 0.01 us  [shards(): rows = lax.all_to_all(rows, AXES, 0, 0, axis_index_groups=gather_groups())]
    all_to_all x1, starting transfers between devices: 10.2 us -> 12.8 us  [shards(): rows = lax.all_to_all(rows, AXES, 0, 0, axis_index_groups=gather_groups())]
  transfers between devices with their start and end apart: 1 -> 1, of which waited for: 1 -> 0; matrix products, arithmetic and copies ran while one was open for 0% -> 0% of each run, Pallas kernels for 6% -> 7%
where the time goes in v4:
time: 46.6 us; the launch traced here: 45.9 us
  blocking collectives  19.9 us (43%)
  starting transfers between devices  12.8 us (27%)
  Pallas kernels  11.1 us (24%)
  local copies, waits for them, and re-layouts  1.96 us (4%)
    all_to_all x1, blocking collectives, shards(): lax.all_to_all(parts, AXES, 0, 0, axis_index_groups=scatter_groups())  19.9 us
    all_to_all x1, starting transfers between devices, shards(): rows = lax.all_to_all(rows, AXES, 0, 0, axis_index_groups=gather_groups())  12.8 us
    pallas_call x2, Pallas kernels, run(): pl.pallas_call(functools.partial(body, device_place), in_specs=in_specs,...  11.1 us
    broadcast_in_dim x1, local copies, waits for them, and re-layouts, shards(): rows = jnp.broadcast_to(rows, (16, 16, 128))  1.36 us
  transfers between devices with their start and end apart: 1, of which 0 were waited for; matrix products, arithmetic and copies ran while one was open for 0% of the time, Pallas kernels for 7%

profile of v4, /device:TPU:1, one launch (start us, length us, event | category | flops | bytes accessed | tf_op | source)
XLA Modules:
  0.0 45.9 jit_solution(10908163972096182115)
XLA Ops:
  0.0 1.4 %broadcast_in_dim.8 = f32[16,16,128]{2,1,0:T(8,128)} broadcast(f32[16,128]{1,0:T(8,128)} %bitcast.3), dimensions={1,2} | broadcast | bytes 139264 | tf_op jit(solution)/shard_map/broadcast_in_dim | solution.py:734
  1.4 12.8 %all-to-all-start = ((f32[16,16,128]{2,1,0:T(8,128)}), f32[16,16,128]{2,1,0:T(8,128)S(1)}, u32[]{:S(2)}, u32[]{:S(2)}) async-start(f32[16,16,128]{2,1,0:T(8,128)} %broadcast_in_dim.8), calls=%async_computation | async-start | bytes 262144 | tf_op jit(solution)/shard_map/all_to_all | solution.py:735
  14.1 3.2 %shard_map.17 = (bf16[44,256,128]{2,1,0:T(8,128)(2,1)S(1)}, f32[64,8,128]{2,1,0:T(8,128)S(1)}, bf16[20,256,128]{2,1,0:T(8,128)(2,1)}, f32[1200,8,128]{2,1,0:T(8,128)}) custom-call(), custom_call_target="tpu_custom_call" | custom-call | tf_op jit(solution)/shard_map/pallas_call | solution.py:670
  17.3 0.0 all-to-all-done.rows_ref
  17.3 8.0 %shard_map.18 = f32[128,128]{1,0:T(8,128)S(1)} custom-call(f32[16,16,128]{2,1,0:T(8,128)S(1)} %all-to-all-done.rows_ref, bf16[44,256,128]{2,1,0:T(8,128)(2,1)S(1)} %get-tuple-element.9.near_ref, f32[64,8,128]{2,1,0:T(8,128)S(1)} %get-tuple-element.10.turn_ref, bf16[20,256,128]{2,1,0:T(8,128)(2,1)} %get-tuple-element.11.far_ref, ...), custom_call_target="tpu_custom_call" | custom-call | tf_op jit(solution)/shard_map/pallas_call | solution.py:670
  25.3 19.9 %all_to_all.10 = f32[32,4,128]{2,1,0:T(4,128)S(1)} all-to-all(f32[32,4,128]{2,1,0:T(4,128)S(1)} %bitcast.2), channel_id=1, replica_groups={{268,264,332,328,396,392,460,456,12,8,76,72,140,136,204,200,260,256,324..., dimensions={0} | all-to-all | bytes 131072 | tf_op jit(solution)/shard_map/all_to_all | solution.py:737
  45.3 0.6 %reshape.9 = f32[2,256]{1,0:T(2,128)} reshape(f32[4,128]{1,0:T(4,128)S(1)} %reduce_sum.9) | data formatting | bytes 4096 | tf_op jit(solution)/shard_map/reshape | solution.py:738
  (1 shorter events, 0.0 us)
Async XLA Ops:
  1.4 16.0 %all-to-all-start = ((f32[16,16,128]{2,1,0:T(8,128)}), f32[16,16,128]{2,1,0:T(8,128)S(1)}, u32[]{:S(2)}, u32[]{:S(2)}) async-start(f32[16,16,128]{2,1,0:T(8,128)} %broadcast_in_dim.8), calls=%async_computation | async-start | bytes 262144 | tf_op jit(solution)/shard_map/all_to_all | solution.py:735

commit v5 on v4

--- a/solution.py
+++ b/solution.py
@@ -153,12 +153,12 @@
 
 
 NEAR = 11
-STRETCHES = ((7, 11), (11, 15), (15, 19))
+STRETCHES = ((0, 7), (7, 11), (11, 15), (15, 19))
 
 
 def stretch(k, table, held, sem, out):
     low, high = STRETCHES[k]
-    far = table.at[pl.ds((low - 7) * 100, (high - low) * 100)]
+    far = table.at[pl.ds(low * 100, (high - low) * 100)]
     near = held.at[pl.ds(low * 100, (high - low) * 100)]
     return pltpu.make_async_copy(near, far, sem) if out else pltpu.make_async_copy(far, near, sem)
 
@@ -320,7 +320,7 @@
         return carry
 
     lax.fori_loop(NEAR, 16, far_wave, 0, unroll=True)
-    save_far = pltpu.make_async_copy(far_s, far_ref, sems.at[3])
+    save_far = pltpu.make_async_copy(far_s, far_ref, sems.at[4])
     save_far.start()
 
     def held(index, b0, b1, factor):
@@ -328,8 +328,9 @@
             table_s[index * 100 + (b0 * 5 + b1) * 4 + k] = factor[k]
 
     saves = []
-    for i, level in enumerate(plan(a, b, sub, (g0, g1, g2))[8:]):
-        point = turning(level, 0, p_ref, q_ref, s_ref, held)
+    part = jnp.where(bit2 == 1, 1.0, -1.0)
+    for i, level in enumerate(plan(a, b, sub, (g0, g1, g2))[2:]):
+        point = turning(level, 0, p_ref, q_ref, s_ref, held, part if i in (1, 2, 3) else None)
 
         def across(b1, carry, point=point):
             for b0 in range(5):
@@ -337,8 +338,8 @@
             return carry
 
         lax.fori_loop(0, 5, across, 0, unroll=True)
-        if i % 2:
-            k = i // 2
+        if i in (5, 7, 9, 11):
+            k = (i - 5) // 2
             saves.append(stretch(k, table_ref, table_s, sems.at[k], True))
             saves[-1].start()
     lax.fori_loop(0, NEAR, near_wave, 0, unroll=True)
@@ -348,9 +349,9 @@
 
 
 def kernel(where, rows_ref, near_ref, turn_ref, far_ref, table_ref, out_ref, v_ref, leaf_ref, wa_ref, wb_ref, x_ref, far_s, table_s, first_s, p_ref, q_ref, s_ref, sems):
-    load_far = pltpu.make_async_copy(far_ref, far_s, sems.at[3])
+    load_far = pltpu.make_async_copy(far_ref, far_s, sems.at[4])
     load_far.start()
-    loads = [stretch(k, table_ref, table_s, sems.at[k], False) for k in range(3)]
+    loads = [stretch(k, table_ref, table_s, sems.at[k], False) for k in range(4)]
     for load in loads:
         load.start()
     a, b, lane, sub, kept = places(where)
@@ -367,7 +368,7 @@
     part = jnp.where(upper, 1.0, -1.0)
 
     points = []
-    for i, level in enumerate(plan(a, b, sub, kept)[:8]):
+    for i, level in enumerate(plan(a, b, sub, kept)[:2]):
         point = turning(
             level, i, p_ref, q_ref, s_ref, hold_first if i < 2 else hold, part if i in (3, 4, 5) else None
         )
@@ -577,6 +578,7 @@
         lambda i, side, j: float(CHILD[side][i, j]),
         writer(wa_ref, lambda m: 0),
     )
+    loads[0].wait()
     def pack(m, i0, i1, b2, totals):
         re, im = totals
         both = jnp.where(upper, im, re) + pltpu.roll(jnp.where(upper, re, im), 4, 0)
@@ -608,7 +610,7 @@
         0, line, 2, reader(wb_ref, 0, order), turner(lambda m: 5 + m, order), lower,
         writer(wa_ref, lambda m: m, order),
     )
-    loads[0].wait()
+    loads[1].wait()
     order = flipped(1, b >> 3 & 1)
     for k6 in range(2):
         merge(
@@ -617,8 +619,8 @@
             writer(wb_ref, (lambda k6: lambda m: 2 * k6 + m)(k6), order),
         )
 
-    loads[1].wait()
     loads[2].wait()
+    loads[3].wait()
     scale = 1.0 / math.sqrt(GC * NF * N_INLINE * N_XLINE)
     for k67 in range(4):
         read = reader(wb_ref, k67)
@@ -683,7 +685,7 @@
             jax.ShapeDtypeStruct((NEAR * GC, 256, 128), BF16),
             jax.ShapeDtypeStruct((64, 8, 128), F32),
             pltpu.HBM(((16 - NEAR) * GC, 256, 128), BF16),
-            pltpu.HBM((1200, 8, 128), F32),
+            pltpu.HBM((1900, 8, 128), F32),
         ],
         out_specs=[in_vmem(), in_vmem(), in_hbm(), in_hbm()],
         scratch_shapes=[
@@ -693,7 +695,7 @@
             pltpu.VMEM((1, 5, 8, 128), F32),
             pltpu.VMEM((1, 5, 8, 128), F32),
             pltpu.VMEM((1, 5, 8, 128), F32),
-            pltpu.SemaphoreType.DMA((4,)),
+            pltpu.SemaphoreType.DMA((5,)),
         ],
         compiler_params=pltpu.CompilerParams(vmem_limit_bytes=14 << 20),
     )
@@ -723,7 +725,7 @@
             pltpu.VMEM((8, 5, 8, 128), F32),
             pltpu.VMEM((8, 5, 8, 128), F32),
             pltpu.VMEM((8, 5, 8, 128), F32),
-            pltpu.SemaphoreType.DMA((4,)),
+            pltpu.SemaphoreType.DMA((5,)),
         ],
         compiler_params=pltpu.CompilerParams(vmem_limit_bytes=20 << 20),
     )

time: 46.6 us -> 48.2 us (1.034); the launches traced: 45.9 us -> 48 us
  Pallas kernels: 11.1 us -> 12.9 us
    pallas_call x2, Pallas kernels: 11.1 us -> 12.9 us  [run(): pl.pallas_call(functools.partial(body, device_place), in_specs=in_specs,...]
  transfers between devices with their start and end apart: 1 -> 1, of which waited for: 0 -> 0; matrix products, arithmetic and copies ran while one was open for 0% -> 0% of each run, Pallas kernels for 7% -> 9%
where the time goes in v5:
time: 48.2 us; the launch traced here: 48 us
  blocking collectives  20.3 us (42%)
  Pallas kernels  12.9 us (27%)
  starting transfers between devices  12.8 us (27%)
  local copies, waits for them, and re-layouts  1.95 us (4%)
    all_to_all x1, blocking collectives, shards(): lax.all_to_all(parts, AXES, 0, 0, axis_index_groups=scatter_groups())  20.3 us
    pallas_call x2, Pallas kernels, run(): pl.pallas_call(functools.partial(body, device_place), in_specs=in_specs,...  12.9 us
    all_to_all x1, starting transfers between devices, shards(): rows = lax.all_to_all(rows, AXES, 0, 0, axis_index_groups=gather_groups())  12.8 us
    broadcast_in_dim x1, local copies, waits for them, and re-layouts, shards(): rows = jnp.broadcast_to(rows, (16, 16, 128))  1.35 us
  transfers between devices with their start and end apart: 1, of which 0 were waited for; matrix products, arithmetic and copies ran while one was open for 0% of the time, Pallas kernels for 9%

profile of v5, /device:TPU:1, one launch (start us, length us, event | category | flops | bytes accessed | tf_op | source)
XLA Modules:
  0.0 48.0 jit_solution(14425355212753026128)
XLA Ops:
  0.0 1.4 %broadcast_in_dim.8 = f32[16,16,128]{2,1,0:T(8,128)} broadcast(f32[16,128]{1,0:T(8,128)} %bitcast.3), dimensions={1,2} | broadcast | bytes 139264 | tf_op jit(solution)/shard_map/broadcast_in_dim | solution.py:736
  1.4 12.8 %all-to-all-start = ((f32[16,16,128]{2,1,0:T(8,128)}), f32[16,16,128]{2,1,0:T(8,128)S(1)}, u32[]{:S(2)}, u32[]{:S(2)}) async-start(f32[16,16,128]{2,1,0:T(8,128)} %broadcast_in_dim.8), calls=%async_computation | async-start | bytes 262144 | tf_op jit(solution)/shard_map/all_to_all | solution.py:737
  14.1 4.5 %shard_map.17 = (bf16[44,256,128]{2,1,0:T(8,128)(2,1)S(1)}, f32[64,8,128]{2,1,0:T(8,128)S(1)}, bf16[20,256,128]{2,1,0:T(8,128)(2,1)}, f32[1900,8,128]{2,1,0:T(8,128)}) custom-call(), custom_call_target="tpu_custom_call" | custom-call | tf_op jit(solution)/shard_map/pallas_call | solution.py:672
  18.7 0.0 all-to-all-done.rows_ref
  18.7 8.4 %shard_map.18 = f32[128,128]{1,0:T(8,128)S(1)} custom-call(f32[16,16,128]{2,1,0:T(8,128)S(1)} %all-to-all-done.rows_ref, bf16[44,256,128]{2,1,0:T(8,128)(2,1)S(1)} %get-tuple-element.9.near_ref, f32[64,8,128]{2,1,0:T(8,128)S(1)} %get-tuple-element.10.turn_ref, bf16[20,256,128]{2,1,0:T(8,128)(2,1)} %get-tuple-element.11.far_ref, ...), custom_call_target="tpu_custom_call" | custom-call | tf_op jit(solution)/shard_map/pallas_call | solution.py:672
  27.1 20.3 %all_to_all.10 = f32[32,4,128]{2,1,0:T(4,128)S(1)} all-to-all(f32[32,4,128]{2,1,0:T(4,128)S(1)} %bitcast.2), channel_id=1, replica_groups={{268,264,332,328,396,392,460,456,12,8,76,72,140,136,204,200,260,256,324..., dimensions={0} | all-to-all | bytes 131072 | tf_op jit(solution)/shard_map/all_to_all | solution.py:739
  47.4 0.6 %reshape.9 = f32[2,256]{1,0:T(2,128)} reshape(f32[4,128]{1,0:T(4,128)S(1)} %reduce_sum.9) | data formatting | bytes 4096 | tf_op jit(solution)/shard_map/reshape | solution.py:740
  (1 shorter events, 0.0 us)
Async XLA Ops:
  1.4 17.3 %all-to-all-start = ((f32[16,16,128]{2,1,0:T(8,128)}), f32[16,16,128]{2,1,0:T(8,128)S(1)}, u32[]{:S(2)}, u32[]{:S(2)}) async-start(f32[16,16,128]{2,1,0:T(8,128)} %broadcast_in_dim.8), calls=%async_computation | async-start | bytes 262144 | tf_op jit(solution)/shard_map/all_to_all | solution.py:737
